TPU v7x, 128 devices: a whole 4x4x4 slice. The times are simulated.
128 devices in a mesh: row: 8 (over y, core), col: 16 (over z, x).
Axes of the slice: x: 4, y: 4, z: 4, core: 2. Of those that a mesh axis runs over, the one named last changes fastest.
Arguments:
- matrix: float32 [8, 8, 256, 4, 16, 256], P(None, 'row', None, None, 'col'), may hold values from -10 to 20, as said below
Outputs:
- factored: float32 [8, 8, 256, 4, 16, 256], P(None, 'row', None, None, 'col')
Inputs may be any that keep to these rules, and one draw needn't show every extreme that they name: matrix is symmetric, and its leading 2 * 256 rows and columns form a positive definite block.
All inputs are finite; a program needn't handle non-finite values.
Results may differ from a plain program's by a relative error of at most 0.0001.
Values sent between devices are 32-bit elements; how exact they have to be, the bound alone decides.
No kernel may reach another device: no remote copies, remote signals or barrier semaphores. Data moves between devices by JAX's collectives and lax.ppermute only.
A program may use at most 128 MiB of HBM per device.

v0:
```python
import jax
import jax.numpy as jnp
from jax import lax
from jax.sharding import PartitionSpec as P

STEPS = 2


def broadcast(value, axis, root):
    return lax.dynamic_index_in_dim(lax.all_gather(value, axis), root, 0, keepdims=False)


def broadcast_2(value, axis, source):
    kept = jnp.where(lax.axis_index(axis) == source, value, 0).astype(value.dtype)
    return lax.psum(kept, axis)


def local(matrix):
    block_rows, _, tile_edge, block_cols, _, _ = matrix.shape
    blocks = matrix.reshape(block_rows, tile_edge, block_cols, tile_edge)
    row_count = lax.axis_size("row")
    col_count = lax.axis_size("col")
    here_row = lax.axis_index("row")
    here_col = lax.axis_index("col")
    row_ids = jnp.arange(block_rows) * row_count + here_row
    col_ids = jnp.arange(block_cols) * col_count + here_col
    identity = jnp.eye(tile_edge, dtype=jnp.float32)

    def panels(blocks, section_at):
        diag_row = section_at // row_count
        diag_col = section_at // col_count
        diagonal = broadcast(blocks[diag_row, :, diag_col, :], "row", section_at % row_count)
        diag_factor = jnp.linalg.cholesky(diagonal)
        diag_inverse = jax.scipy.linalg.solve_triangular(diag_factor, identity, lower=True)
        factor_panel = jnp.einsum(
            "anb,cb->anc", blocks[:, :, diag_col, :], diag_inverse, precision=lax.Precision.HIGHEST
        )
        factor_panel = jnp.where(
            (row_ids > section_at)[:, None, None], factor_panel, jnp.zeros_like(factor_panel)
        )
        colvals = factor_panel + jnp.where(
            (row_ids == section_at)[:, None, None], diag_factor[None], jnp.zeros_like(factor_panel)
        )
        row_panel = broadcast_2(factor_panel, "col", section_at % col_count)
        source = broadcast_2(row_panel, "row", here_col % row_count)
        picked = jnp.arange(block_cols) * (col_count // row_count) + here_col // row_count
        col_panel = jnp.take(source, picked, axis=0)
        return (row_panel, col_panel, colvals)

    def trailing(blocks, pending, start, stop):
        if stop <= start:
            return blocks
        row_panel, col_panel, _ = pending
        update = jnp.einsum(
            "anb,cmb->ancm", row_panel, col_panel[start:stop], precision=lax.Precision.HIGHEST
        )
        return blocks.at[:, :, start:stop, :].add(-update)

    def finish(blocks, section_at, pending):
        diag_col = section_at // col_count
        on_col = here_col == section_at % col_count
        column = jnp.where(on_col, pending[2], blocks[:, :, diag_col, :])
        blocks = blocks.at[:, :, diag_col, :].set(column)
        zero_row = (row_ids == section_at)[:, None, None, None] & (col_ids > section_at)[
            None, None, :, None
        ]
        return jnp.where(zero_row, jnp.zeros_like(blocks), blocks)

    pending = panels(blocks, 0)
    for section_at in range(STEPS):
        if section_at + 1 < STEPS:
            next_col = (section_at + 1) // col_count
            blocks = trailing(blocks, pending, next_col, next_col + 1)
            blocks = finish(blocks, section_at, pending)
            upcoming = panels(blocks, section_at + 1)
            blocks = trailing(blocks, pending, 0, next_col)
            blocks = trailing(blocks, pending, next_col + 1, block_cols)
            pending = upcoming
        else:
            blocks = trailing(blocks, pending, 0, block_cols)
            blocks = finish(blocks, section_at, pending)
    return blocks.reshape(matrix.shape)


def solution(mesh):
    in_specs = (P(None, "row", None, None, "col", None),)
    out_specs = P(None, "row", None, None, "col", None)
    return jax.shard_map(local, mesh=mesh, in_specs=in_specs, out_specs=out_specs, check_vma=False)
```

profile of v0, /device:TPU:0, one launch (start us, length us, event | category | flops | bytes accessed | tf_op | source)
XLA Modules:
  0.0 581.7 jit_solution(6778422841316692927)
XLA Ops:
  6.5 5.0 copy.50
  11.6 3.4 copy-done.1
  15.8 27.9 %all-gather.5.cloned.1.call-done = f32[8,256,1,256]{3,1,2,0:T(8,128)} async-done(((f32[1,256,1,256]{3,1,2,0:T(8,128)}), f32[8,256,1,256]{3,1,2,0:T(8,128)}) %all-gather.5.cloned.1.call-update) | async-done | bytes 2097168 | tf_op jit(solution)/shard_map/all_gather | solution.py:10
  45.7 11.7 %cholesky.130 = f32[128,128]{1,0:T(8,128)S(1)} custom-call(f32[128,128]{1,0:T(8,128)S(1)} %cholesky.194), custom_call_target="Cholesky" | custom-call | tf_op jit(solution)/shard_map/jit(cholesky)/cholesky | solution.py:33
  57.5 9.8 %custom-call.13 = f32[1,128,128]{1,2,0:T(8,128)S(1)} custom-call(f32[1,128,128]{2,1,0:T(8,128)S(1)} %get-tuple-element.123), custom_call_target="InvertDiagBlocksLowerTriangular" | custom-call | tf_op jit(solution)/shard_map/jit(cholesky)/cholesky | solution.py:33
  67.8 11.7 %cholesky.147 = f32[128,128]{1,0:T(8,128)S(1)} custom-call(f32[128,128]{1,0:T(8,128)S(1)} %convolution_subtract_fusion.3), custom_call_target="Cholesky" | custom-call | tf_op jit(solution)/shard_map/jit(cholesky)/cholesky | solution.py:33
  82.4 4.3 while.10
  86.6 19.7 %custom-call.14 = f32[2,128,128]{1,2,0:T(8,128)S(1)} custom-call(f32[2,128,128]{2,1,0:T(8,128)S(1)} %get-tuple-element.90), custom_call_target="InvertDiagBlocksLowerTriangular" | custom-call | tf_op jit(solution)/shard_map/jit(_solve_triangular)/triangular_solve | solution.py:34
  107.2 5.4 bitcast_select_fusion
  112.7 91.8 %all-reduce.6.cloned.1.call-done = f32[8,256,256]{2,1,0:T(8,128)} async-done(((f32[8,256,256]{2,1,0:T(8,128)}), f32[8,256,256]{2,1,0:T(8,128)}) %all-reduce.6.cloned.1.call-update) | async-done | bytes 2097168 | tf_op jit(solution)/shard_map/psum | solution.py:15
  204.5 3.1 broadcast_select_fusion.2
  207.8 64.5 %all-reduce.8.cloned.1.call-done = f32[8,256,256]{2,1,0:T(8,128)} async-done(((f32[8,256,256]{2,1,0:T(8,128)}), f32[8,256,256]{2,1,0:T(8,128)}) %all-reduce.8.cloned.1.call-update) | async-done | bytes 2097168 | tf_op jit(solution)/shard_map/psum | solution.py:15
  272.3 2.2 gather_fusion
  274.7 1.4 slice-done
  276.1 3.2 bitcast_dynamic-update-slice_fusion.3
  279.3 1.7 bitcast_dynamic-update-slice_fusion.2
  281.0 4.2 broadcast_select_fusion
  285.2 3.4 copy-done
  289.8 24.6 %all-gather.7.cloned.1.call-done = f32[8,256,1,256]{3,1,2,0:T(8,128)} async-done(((f32[1,256,1,256]{3,1,2,0:T(8,128)}), f32[8,256,1,256]{3,1,2,0:T(8,128)}) %all-gather.7.cloned.1.call-update) | async-done | bytes 2097168 | tf_op jit(solution)/shard_map/all_gather | solution.py:10
  316.6 11.7 %cholesky.164 = f32[128,128]{1,0:T(8,128)S(1)} custom-call(f32[128,128]{1,0:T(8,128)S(1)} %cholesky.197), custom_call_target="Cholesky" | custom-call | tf_op jit(solution)/shard_map/jit(cholesky)/cholesky | solution.py:33
  328.3 9.8 %custom-call.15 = f32[1,128,128]{1,2,0:T(8,128)S(1)} custom-call(f32[1,128,128]{2,1,0:T(8,128)S(1)} %get-tuple-element.119), custom_call_target="InvertDiagBlocksLowerTriangular" | custom-call | tf_op jit(solution)/shard_map/jit(cholesky)/cholesky | solution.py:33
  338.6 11.7 %cholesky.181 = f32[128,128]{1,0:T(8,128)S(1)} custom-call(f32[128,128]{1,0:T(8,128)S(1)} %convolution_subtract_fusion.2), custom_call_target="Cholesky" | custom-call | tf_op jit(solution)/shard_map/jit(cholesky)/cholesky | solution.py:33
  353.8 4.2 while.11
  358.0 19.7 %custom-call.16 = f32[2,128,128]{1,2,0:T(8,128)S(1)} custom-call(f32[2,128,128]{2,1,0:T(8,128)S(1)} %get-tuple-element.91), custom_call_target="InvertDiagBlocksLowerTriangular" | custom-call | tf_op jit(solution)/shard_map/jit(_solve_triangular)/triangular_solve | solution.py:34
  378.6 5.4 select_select_fusion
  384.1 91.8 %all-reduce.10.cloned.1.call-done = f32[8,256,256]{2,1,0:T(8,128)} async-done(((f32[8,256,256]{2,1,0:T(8,128)}), f32[8,256,256]{2,1,0:T(8,128)}) %all-reduce.10.cloned.1.call-update) | async-done | bytes 2097168 | tf_op jit(solution)/shard_map/psum | solution.py:15
  475.8 3.1 broadcast_select_fusion.1
  480.2 9.1 %fusion = f32[8,256,4,256]{3,1,0,2:T(8,128)} fusion(f32[8,256,4,256]{3,1,0,2:T(8,128)} %copy-done, f32[8,256,256]{2,1,0:T(8,128)S(1)} %copy-done.2, f32[4,256,256]{2,1,0:T(8,128)S(1)} %copy-done.7), kind=kOutput, calls=%fused_computation.10 | convolution fusion | flops 4834983936 | bytes 15466496 | tf_op jit(solution)/shard_map/anb,cmb->ancm/dot_general | solution.py:54
  489.3 54.3 %all-reduce.12.cloned.1.call-done = f32[8,256,256]{2,1,0:T(8,128)} async-done(((f32[8,256,256]{2,1,0:T(8,128)}), f32[8,256,256]{2,1,0:T(8,128)}) %all-reduce.12.cloned.1.call-update) | async-done | bytes 2097168 | tf_op jit(solution)/shard_map/psum | solution.py:15
  543.7 2.2 gather_fusion.1
  545.9 10.5 %negate_add_fusion = f32[8,256,4,256]{3,1,0,2:T(8,128)S(1)} fusion(f32[8,256,4,256]{3,1,0,2:T(8,128)} %fusion, f32[8,256,256]{2,1,0:T(8,128)S(1)} %copy-done.3, f32[4,256,256]{2,1,0:T(8,128)S(1)} %gather_fusion.1, pred[4]{0:T(512)(128)(4,1)S(1)} %compare_and_fusion), kind=kOutput, calls=%fused_computation.8 | convolution fusion | flops 6446907392 | bytes 19922948 | tf_op jit(solution)/shard_map/anb,cmb->ancm/dot_general | solution.py:54
  558.4 16.3 %copy.35 = f32[8,1,256,4,1,256]{5,4,3,2,1,0:T(1,128)} copy(f32[8,1,256,4,1,256]{5,2,0,3,4,1:T(8,128)S(1)} %select_bitcast_fusion) | data formatting | bytes 16777216 | tf_op jit(solution)/shard_map/reshape | solution.py:82
  (92 shorter events, 24.3 us)
Async XLA Ops:
  6.5 37.1 %all-gather.5.cloned.1.call-start = ((), (), s32[]{:S(2)}) async-start(), calls=%async_computation.4 | async-start | bytes 2359296 | tf_op jit(solution)/shard_map/all_gather | solution.py:10
  11.5 3.4 copy-start.1
  15.7 188.8 %all-reduce.6.cloned.1.call-start = ((), (), s32[]{:S(2)}) async-start(), calls=%async_computation | async-start | bytes 4194304 | tf_op jit(solution)/shard_map/psum | solution.py:15
  112.6 159.7 %all-reduce.8.cloned.1.call-start = ((), (), s32[]{:S(2)}) async-start(), calls=%async_computation.1 | async-start | bytes 4194304 | tf_op jit(solution)/shard_map/psum | solution.py:15
  207.6 106.8 %all-gather.7.cloned.1.call-start = ((), (), s32[]{:S(2)}) async-start(), calls=%async_computation.5 | async-start | bytes 2359296 | tf_op jit(solution)/shard_map/all_gather | solution.py:10
  207.8 66.9 %copy-start.2 = (f32[8,256,256]{2,1,0:T(8,128)S(1)}, f32[8,256,256]{2,1,0:T(8,128)}, u32[]{:S(2)}) copy-start(f32[8,256,256]{2,1,0:T(8,128)} %all-reduce.6.cloned.1.call-done) | copy-start | bytes 6291460
  274.5 1.6 slice-start
  276.1 3.2 copy-start.6
  276.1 3.2 copy-start.4
  276.1 3.2 copy-start.8
  285.2 3.4 copy-start
  289.4 186.5 %all-reduce.10.cloned.1.call-start = ((), (), s32[]{:S(2)}) async-start(), calls=%async_computation.2 | async-start | bytes 4194304 | tf_op jit(solution)/shard_map/psum | solution.py:15
  384.0 159.7 %all-reduce.12.cloned.1.call-start = ((), (), s32[]{:S(2)}) async-start(), calls=%async_computation.3 | async-start | bytes 4194304 | tf_op jit(solution)/shard_map/psum | solution.py:15
  479.0 1.2 copy-start.7
  489.3 56.6 %copy-start.3 = (f32[8,256,256]{2,1,0:T(8,128)S(1)}, f32[8,256,256]{2,1,0:T(8,128)}, u32[]{:S(2)}) copy-start(f32[8,256,256]{2,1,0:T(8,128)} %all-reduce.10.cloned.1.call-done) | copy-start | bytes 6291460
  545.9 10.6 %copy-start.5 = (f32[8,256,256]{2,1,0:T(8,128)S(1)}, f32[8,256,256]{2,1,0:T(8,128)}, u32[]{:S(2)}) copy-start(f32[8,256,256]{2,1,0:T(8,128)} %get-tuple-element.133) | copy-start | bytes 6291460
  545.9 10.6 %copy-start.9 = (f32[256,256]{1,0:T(8,128)S(1)}, f32[256,256]{1,0:T(8,128)}, u32[]{:S(2)}) copy-start(f32[256,256]{1,0:T(8,128)} %get-tuple-element.109) | copy-start | bytes 786436
Sparse Core Ops, SparseCore 0:
  15.8 27.7 all-gather.4
  112.7 91.6 all-reduce.5
  207.7 64.5 all-reduce.7
  289.5 24.9 all-gather.6
  384.1 91.6 all-reduce.9
  479.1 64.5 all-reduce.11
where the time goes:
time: 591 us; the launch traced here: 582 us
  waiting for transfers between devices  355 us (60%)
  other arithmetic  126 us (21%)
  local copies, waits for them, and re-layouts  46.7 us (8%)
  matrix products  36.3 us (6%)
  between operations  16.7 us (3%)
    psum x4, waiting for transfers between devices, broadcast_2(): return lax.psum(kept, axis)  302 us
    another operation x13, other arithmetic, panels(): diag_factor = jnp.linalg.cholesky(diagonal)  68.7 us
    all_gather x2, waiting for transfers between devices, broadcast(): lax.all_gather(value, axis)  52.5 us
    another operation x5, other arithmetic, panels(): jax.scipy.linalg.solve_triangular(diag_factor, identity, lower=True)  40.8 us
    dot_general x3, matrix products, trailing(): jnp.einsum('anb,cmb->ancm', row_panel, col_panel[start:stop], precision=l...  22.9 us
    reshape x1, local copies, waits for them, and re-layouts, local(): return blocks.reshape(matrix.shape)  16.3 us
    unnamed x23, local copies, waits for them, and re-layouts  13.2 us
  transfers between devices with their start and end apart: 6, of which 6 were waited for; matrix products, arithmetic and copies ran while one was open for 2% of the time, Pallas kernels for 0%

commit v1 on v0

v1 whole, which is shorter than its diff:
```python
import jax
import jax.numpy as jnp
from jax import lax
from jax.experimental import pallas as pl
from jax.experimental.pallas import tpu as pltpu
from jax.sharding import PartitionSpec as P


F32 = jnp.float32
BF16 = jnp.bfloat16
NB = 256
HALF = 128
W = 512
GROUP = 8
HIGH = lax.Precision.HIGHEST
VMEM = pl.BlockSpec(memory_space=pltpu.VMEM)
AXES = ("row", "col")
NY, NK, NZ, NX = 4, 2, 4, 4
FLOPS_US = 1_000_000_000


def device(y, k, z, x):
    return (y * NK + k) * (NZ * NX) + z * NX + x


def grid_devices():
    for y in range(NY):
        for k in range(NK):
            for z in range(NZ):
                for x in range(NX):
                    yield y, k, z, x


def swap(value, y=0, k=0, z=0, x=0, only=None):
    pairs = []
    for dev in grid_devices():
        if only is None or only(*dev):
            target = (dev[0] ^ y, dev[1] ^ k, dev[2] ^ z, dev[3] ^ x)
            pairs.append((device(*dev), device(*target)))
    return lax.ppermute(value, AXES, pairs)


def scatter(value, part):
    pairs = []
    for k in range(2):
        for col in range(NZ * NX):
            row = col % (NY * NK)
            y, core = row // NK, row % NK
            z = 2 * (col // (NY * NK)) + k
            x = (col % NX) ^ part
            pairs.append((k * (NZ * NX) + col, device(y, core, z, x)))
    return lax.ppermute(value, AXES, pairs)


def nt(a, b):
    return lax.dot_general(a, b, (((1,), (1,)), ((), ())), precision=HIGH, preferred_element_type=F32)


def nn(a, b):
    return lax.dot_general(a, b, (((1,), (0,)), ((), ())), precision=HIGH, preferred_element_type=F32)


def split(value):
    hi = value.astype(BF16)
    lo = (value - hi.astype(F32)).astype(BF16)
    return hi, lo


def extract_kernel(a_ref, corner_ref, whole_ref, *part_refs):
    k = lax.axis_index("row") % NK
    x = lax.axis_index("col") % NX

    def fill(*tiles):
        for at, (i, j) in enumerate(tiles):
            corner_ref[at] = a_ref[pl.ds(i * HALF * 8 + j, HALF, stride=8), :]

    pl.when(k == x)(lambda: fill((0, 0), (1, 0), (1, 1)))
    pl.when((k != x) & (k == 0))(lambda: fill((0, 1), (1, 1), (1, 1)))
    pl.when((k != x) & (k == 1))(lambda: fill((0, 0), (0, 1), (0, 1)))
    for b in range(4):
        for h in range(2):
            value = a_ref[pl.ds(2 * b + h, NB, stride=8), :]
            whole_ref[b, :, h * HALF:(h + 1) * HALF] = value
            part_refs[b][:, h * HALF:(h + 1) * HALF] = value


def extract(view):
    shapes = [(3, HALF, HALF), (4, NB, NB)] + [(NB, NB)] * 4
    return pl.pallas_call(
        extract_kernel,
        grid=(1,),
        in_specs=[pl.BlockSpec((NB * 8, HALF), lambda i: (0, 0))],
        out_specs=[VMEM] * 6,
        out_shape=[jax.ShapeDtypeStruct(shape, F32) for shape in shapes],
        name="extract",
    )(view)


def prep_kernel(s0, s1, s2, s3, alpha, beta):
    whole = (s0[...] + s1[...]) + (s2[...] + s3[...])
    turned = whole.T
    alpha[...] = turned[:HALF]
    beta[...] = turned[HALF:]


def prep(parts):
    half = jax.ShapeDtypeStruct((HALF, NB), F32)
    return pl.pallas_call(prep_kernel, out_shape=(half, half), name="prep")(*parts)


def factor_diagonal(a_ref, m_ref, u_ref, t_ref):
    rows = lax.broadcasted_iota(jnp.int32, (HALF, HALF), 0)
    cols = lax.broadcasted_iota(jnp.int32, (HALF, HALF), 1)
    m_ref[...] = jnp.where(rows == cols, 1.0, 0.0).astype(F32)
    full = (GROUP, HALF)
    groups = HALF // GROUP
    for step in range(groups):
        base = step * GROUP
        pivot = a_ref[base:base + GROUP, :]
        for k in range(GROUP):
            t_ref[k] = jnp.broadcast_to(pivot[:, base + k:base + k + 1], full)
        s = [[None] * GROUP for _ in range(GROUP)]
        for i in range(GROUP):
            for k in range(i + 1):
                s[i][k] = jnp.broadcast_to(t_ref[k, i:i + 1, :], full)
        low = [[None] * GROUP for _ in range(GROUP)]
        inv_d = [None] * GROUP
        root = [None] * GROUP
        for k in range(GROUP):
            root[k] = lax.rsqrt(s[k][k])
            inv_d[k] = 1.0 / s[k][k]
            for i in range(k + 1, GROUP):
                low[i][k] = s[i][k] * inv_d[k]
            for i in range(k + 1, GROUP):
                for j in range(k + 1, i + 1):
                    s[i][j] = s[i][j] - low[i][k] * s[j][k]
        inv = [[None] * GROUP for _ in range(GROUP)]
        for j in range(GROUP):
            for i in range(j + 1, GROUP):
                total = low[i][j]
                for k in range(j + 1, i):
                    total = total + low[i][k] * inv[k][j]
                inv[i][j] = -total
        weights = []
        for ref, out in ((a_ref, u_ref), (m_ref, m_ref)):
            raw = [jnp.broadcast_to(ref[base + i:base + i + 1, :], full) for i in range(GROUP)]
            z = []
            for i in range(GROUP):
                total = raw[i]
                for k in range(i):
                    total = total + inv[i][k] * raw[k]
                z.append(total)
            scaled = [z[i] * inv_d[i] for i in range(GROUP)]
            w = []
            for k in range(GROUP):
                total = scaled[k]
                for i in range(k + 1, GROUP):
                    total = total + inv[i][k] * scaled[i]
                w.append(total)
            weights.append(w)
            for i in range(GROUP):
                out[base + i:base + i + 1, :] = (z[i] * root[i])[0:1, :]
        for g in range(step + 1, groups):
            at = g * GROUP
            block = a_ref[at:at + GROUP, :]
            other = m_ref[at:at + GROUP, :]
            for k in range(GROUP):
                c = jnp.broadcast_to(block[:, base + k:base + k + 1], full)
                if k == 0:
                    da = c * weights[0][0]
                    dm = c * weights[1][0]
                else:
                    da = da + c * weights[0][k]
                    dm = dm + c * weights[1][k]
            a_ref[at:at + GROUP, :] = block - da
            m_ref[at:at + GROUP, :] = other - dm


def factor_steps(first, last, s_ref, inv_ref, a_ref, m_ref, u_ref, t_ref):
    rows = lax.broadcasted_iota(jnp.int32, (HALF, HALF), 0)
    cols = lax.broadcasted_iota(jnp.int32, (HALF, HALF), 1)
    lower = rows >= cols
    zero = jnp.zeros((HALF, HALF), F32)

    def body(p, carry):
        a_ref[...] = s_ref[p, p]
        factor_diagonal(a_ref, m_ref, u_ref, t_ref)
        inverse = m_ref[...]
        s_ref[p, p] = jnp.where(lower, u_ref[...].T, 0.0)
        for q in range(first, last):

            @pl.when(p == q)
            def _(q=q):
                for j in range(q):
                    total = nn(s_ref[q, j], inv_ref[j, j])
                    for m in range(j + 1, q):
                        total = total + nn(s_ref[q, m], inv_ref[m, j])
                    inv_ref[q, j] = -nn(inverse, total)
                inv_ref[q, q] = inverse
                for j in range(q + 1, 4):
                    inv_ref[q, j] = zero
                for i in range(q + 1, 4):
                    s_ref[i, q] = nt(s_ref[i, q], inverse)
                for i in range(q + 1, 4):
                    for j in range(q + 1, i + 1):
                        s_ref[i, j] = s_ref[i, j] - nt(s_ref[i, q], s_ref[j, q])

        return carry

    lax.fori_loop(first, last, body, 0)


def chol_first_kernel(mine_ref, other_ref, s_ref, inv_ref, *work):
    k = lax.axis_index("row") % NK

    def load(top, bottom):
        s_ref[0, 0] = top[0]
        s_ref[1, 0] = top[1]
        s_ref[1, 1] = top[2]
        s_ref[2, 0] = bottom[3]
        s_ref[2, 1] = bottom[4]
        s_ref[3, 0] = top[3].T
        s_ref[3, 1] = top[4].T
        s_ref[2, 2] = bottom[0]
        s_ref[3, 2] = bottom[1]
        s_ref[3, 3] = bottom[2]

    pl.when(k == 0)(lambda: load(mine_ref, other_ref))
    pl.when(k == 1)(lambda: load(other_ref, mine_ref))
    factor_steps(0, 2, s_ref, inv_ref, *work)


def chol_last_kernel(s_in, inv_in, s_ref, inv_ref, *work):
    s_ref[...] = s_in[...]
    inv_ref[...] = inv_in[...]
    factor_steps(2, 4, s_ref, inv_ref, *work)


TILES = (4, 4, HALF, HALF)


def chol(kernel, operands, flops):
    tiles = jax.ShapeDtypeStruct(TILES, F32)
    return pl.pallas_call(
        kernel,
        in_specs=[VMEM, VMEM],
        out_specs=[VMEM, VMEM],
        out_shape=(tiles, tiles),
        cost_estimate=pl.CostEstimate(flops=flops, bytes_accessed=0, transcendentals=0),
        scratch_shapes=[
            pltpu.VMEM((HALF, HALF), F32),
            pltpu.VMEM((HALF, HALF), F32),
            pltpu.VMEM((HALF, HALF), F32),
            pltpu.VMEM((GROUP, GROUP, HALF), F32),
        ],
    )(*operands)


def three(a, b):
    return (
        jnp.dot(a[0], b[0], preferred_element_type=F32)
        + jnp.dot(a[0], b[1], preferred_element_type=F32)
        + jnp.dot(a[1], b[0], preferred_element_type=F32)
    )


def three_nt(a, b):
    def dot(u, v):
        return lax.dot_general(u, v, (((1,), (1,)), ((), ())), preferred_element_type=F32)

    return dot(a[0], b[0]) + dot(a[0], b[1]) + dot(a[1], b[0])


def finish_kernel(
    a_hbm, al0, al1, al2, al3, be0, be1, be2, be3, mine_ref, other_ref, l_ref, inv_ref,
    out_hbm, buf, lh_ref, c_ref, p_ref, pk_ref, sem_in, sem_out,
):
    row = lax.axis_index("row")
    col = lax.axis_index("col")
    k = row % NK
    z, x = col // NX, col % NX
    alphas = (al0, al1, al2, al3)
    betas = (be0, be1, be2, be3)
    size = NB * 8

    def block_of(t):
        pair, ex = t // 4, t % 4
        return ((z // 2) ^ pair) + 2 * ((x ^ ex) ^ (row % 4))

    def load(t):
        return pltpu.make_async_copy(a_hbm.at[pl.ds(block_of(t) * size, size)], buf.at[t], sem_in.at[t])

    def store(t):
        return pltpu.make_async_copy(buf.at[t], out_hbm.at[pl.ds(block_of(t) * size, size)], sem_out.at[t])

    for t in range(8):
        load(t).start()

    for i in range(4):
        for j in range(4):
            hi, lo = split(inv_ref[i, j])
            at = (slice(i * HALF, (i + 1) * HALF), slice((j % 2) * HALF, (j % 2 + 1) * HALF))
            lh_ref[(j // 2, 0) + at] = hi
            lh_ref[(j // 2, 1) + at] = lo

    def columns(top, bottom):
        for b in range(4):
            x0 = split(top[b])
            x1 = split(bottom[b])
            at = slice(b * NB, (b + 1) * NB)
            up = three((lh_ref[0, 0, :NB, :], lh_ref[0, 1, :NB, :]), x0)
            down = three((lh_ref[0, 0, NB:, :], lh_ref[0, 1, NB:, :]), x0) + three(
                (lh_ref[1, 0, NB:, :], lh_ref[1, 1, NB:, :]), x1
            )
            for i, part in enumerate((up, down)):
                hi, lo = split(part)
                c_ref[i * NB:(i + 1) * NB, at] = hi
                c_ref[W + i * NB:W + (i + 1) * NB, at] = lo
                c_ref[2 * W + i * NB:2 * W + (i + 1) * NB, at] = hi

    pl.when(k == 0)(lambda: columns(mine_ref, other_ref))
    pl.when(k == 1)(lambda: columns(other_ref, mine_ref))

    def panel(even, odd, places):
        first = z % 2
        total = three_nt(split(even), (lh_ref[first, 0], lh_ref[first, 1])) + three_nt(
            split(odd), (lh_ref[1 - first, 0], lh_ref[1 - first, 1])
        )
        for i, (t, half) in enumerate(places):
            at = slice(half * HALF, (half + 1) * HALF)
            part = total[i * HALF:(i + 1) * HALF]
            hi, lo = split(part)
            p_ref[t, at, :] = part
            pk_ref[t, at, 0:W] = hi
            pk_ref[t, at, W:2 * W] = hi
            pk_ref[t, at, 2 * W:3 * W] = lo

    for pair in range(2):
        panel(
            alphas[2 * pair][...].reshape(W, NB),
            alphas[2 * pair + 1][...].reshape(W, NB),
            [(pair * 4 + ex, 0) for ex in range(4)],
        )
    for half in range(2):
        pick = [(ex, pair) for ex in (2 * half, 2 * half + 1) for pair in range(2)]
        panel(
            jnp.concatenate([betas[ex][2 * pair] for ex, pair in pick], axis=0),
            jnp.concatenate([betas[ex][2 * pair + 1] for ex, pair in pick], axis=0),
            [(pair * 4 + ex, 1) for ex, pair in pick],
        )

    def step(u, carry):
        for m in range(2):
            load(2 * u + m).wait()
        left = pk_ref[pl.ds(2 * u, 2)].reshape(2 * NB, 3 * W)
        for b in range(4):
            update = jnp.dot(left, c_ref[:, b * NB:(b + 1) * NB], preferred_element_type=F32)
            for m in range(2):
                for h in range(2):
                    rows = pl.ds(2 * b + h, NB, stride=8)
                    part = update[m * NB:(m + 1) * NB, h * HALF:(h + 1) * HALF]
                    buf[2 * u + m, rows, :] = buf[2 * u + m, rows, :] - part

        for m in range(2):
            t = 2 * u + m
            for c in range(2):
                @pl.when(col == c)
                def _(c=c, t=t):
                    for h in range(2):
                        at = c * NB + h * HALF
                        buf[t, pl.ds(h, NB, stride=8), :] = p_ref[t, :, at:at + HALF]

            for r in range(2):
                @pl.when((row == r) & (block_of(t) == 0))
                def _(r=r, t=t):
                    for s in range(8):
                        buf[t, pl.ds(s, NB, stride=8), :] = jnp.zeros((NB, HALF), F32)
                    for c in range(r + 1):
                        @pl.when(col == c)
                        def _(c=c):
                            for i in range(2):
                                for h in range(2):
                                    if c < r or h <= i:
                                        rows = pl.ds(i * HALF * 8 + h, HALF, stride=8)
                                        buf[t, rows, :] = l_ref[2 * r + i, 2 * c + h]

            store(t).start()
        return carry

    lax.fori_loop(0, 4, step, 0)
    for t in range(8):
        store(t).wait()


def finish(view, alphas, betas, mine, other, lower, inverse):
    hbm = pl.BlockSpec(memory_space=pl.ANY)
    return pl.pallas_call(
        finish_kernel,
        in_specs=[hbm] + [VMEM] * 12,
        out_specs=hbm,
        out_shape=jax.ShapeDtypeStruct(view.shape, F32),
        scratch_shapes=[
            pltpu.VMEM((8, NB * 8, HALF), F32),
            pltpu.VMEM((2, 2, W, NB), BF16),
            pltpu.VMEM((3 * W, 4 * NB), BF16),
            pltpu.VMEM((8, NB, W), F32),
            pltpu.VMEM((8, NB, 3 * W), BF16),
            pltpu.SemaphoreType.DMA((8,)),
            pltpu.SemaphoreType.DMA((8,)),
        ],
        compiler_params=pltpu.CompilerParams(vmem_limit_bytes=56 * 1024 * 1024),
        name="finish",
    )(view, *alphas, *betas, mine, other, lower, inverse)


def after(value, *others):
    return lax.optimization_barrier((value, *others))[0]


def local(matrix):
    row = lax.axis_index("row")
    col = lax.axis_index("col")
    y, k = row // NK, row % NK
    z, x = col // NX, col % NX
    view = matrix.reshape(8 * NB * 8, HALF)

    tiles, blocks, *quarters = extract(view)
    got = [swap(tiles, y=e, only=lambda yy, kk, zz, xx: yy == 0 and zz == 0 and xx < 2) for e in (1, 3, 2)]
    parts = [scatter(quarters[b], b) for b in range(4)]

    tiles = jnp.where(y == 0, tiles, got[0] + got[1] + got[2])
    got = [swap(tiles, z=e, only=lambda yy, kk, zz, xx: zz == 0 and xx < 2) for e in (1, 3, 2)]
    tiles = jnp.where(z == 0, tiles, got[0] + got[1] + got[2])
    late = after(blocks, tiles)
    tiles = [tiles] + [swap(tiles, x=e, only=lambda yy, kk, zz, xx: xx < 2) for e in (1, 2, 3)]

    def pick(j):
        at = x ^ j
        return jnp.where(at == 0, tiles[0], jnp.where(at == 1, tiles[1], jnp.where(at == 2, tiles[2], tiles[3])))

    own = jnp.concatenate([pick(k), pick(1 - k)[:2]], axis=0)
    other = swap(own, k=1)

    alpha, beta = prep(parts)
    along_x = [alpha] + [swap(alpha, x=e) for e in (1, 2, 3)]
    along_z = [beta] + [swap(beta, z=e) for e in (1, 2, 3)]
    along_x = jnp.stack(along_x)
    along_z = jnp.stack(along_z)
    alphas = [along_x] + [swap(along_x, z=e) for e in (1, 2, 3)]
    betas = [along_z] + [swap(along_z, x=e) for e in (1, 2, 3)]

    got = [swap(late, y=e, only=lambda yy, kk, zz, xx: yy == 0) for e in (1, 2, 3)]

    own = after(own, along_x, along_z)
    lower, inverse = chol(chol_first_kernel, (own, other), 12 * FLOPS_US)
    got = lax.optimization_barrier((*got, lower))[:3]
    mine = jnp.where(y == 0, blocks, got[0] + got[1] + got[2])
    mine_other = swap(mine, k=1)
    lower = after(lower, mine)
    lower, inverse = chol(chol_last_kernel, (lower, inverse), 12 * FLOPS_US)
    out = finish(view, alphas, betas, mine, mine_other, lower, inverse)
    return out.reshape(matrix.shape)


def solution(mesh):
    spec = P(None, "row", None, None, "col", None)
    return jax.shard_map(local, mesh=mesh, in_specs=(spec,), out_specs=spec, check_vma=False)
```

time: 591 us -> 159 us (0.27); the launches traced: 582 us -> 156 us
  waiting for transfers between devices: 355 us -> 42.6 us
  other arithmetic: 126 us -> 5.11 us
  starting transfers between devices: 0.61 us -> 57 us
  Pallas kernels: 0 us -> 48.5 us
  local copies, waits for them, and re-layouts: 46.7 us -> 2.46 us
  matrix products: 36.3 us -> 0 us
  between operations: 16.7 us -> 0.59 us
    psum x4 -> x0, waiting for transfers between devices: 302 us -> none  [broadcast_2(): return lax.psum(kept, axis)]
    another operation x18 -> x2, other arithmetic: 109 us -> 1.88 us  [the longest x1 0.94 us: local(): along_z = jnp.stack(along_z)]
    ppermute x0 -> x30, starting transfers between devices: none -> 57 us  [the longest x26 42.1 us: swap(): return lax.ppermute(value, AXES, pairs)]
    all_gather x2 -> x0, waiting for transfers between devices: 52.5 us -> none  [broadcast(): lax.all_gather(value, axis)]
    pallas_call x0 -> x5, Pallas kernels: none -> 48.5 us  [the longest x2 24.5 us: chol(): pl.pallas_call(kernel, in_specs=[VMEM, VMEM], out_specs=[VMEM, VMEM], out...]
    ppermute x0 -> x30, waiting for transfers between devices: none -> 42.6 us  [the longest x26 38.7 us: swap(): return lax.ppermute(value, AXES, pairs)]
    dot_general x5 -> x0, matrix products: 33.6 us -> none  [the longest x3 22.9 us: trailing(): jnp.einsum('anb,cmb->ancm', row_panel, col_panel[start:stop], precision=l...]
    reshape x1 -> x0, local copies, waits for them, and re-layouts: 16.3 us -> none  [local(): return blocks.reshape(matrix.shape)]
  transfers between devices with their start and end apart: 6 -> 30, of which waited for: 6 -> 11; matrix products, arithmetic and copies ran while one was open for 2% -> 3% of each run, Pallas kernels for 0% -> 17%
where the time goes in v1:
time: 159 us; the launch traced here: 156 us
  starting transfers between devices  57 us (36%)
  Pallas kernels  48.5 us (31%)
  waiting for transfers between devices  42.6 us (27%)
  other arithmetic  5.11 us (3%)
  local copies, waits for them, and re-layouts  2.46 us (2%)
    ppermute x26, starting transfers between devices, swap(): return lax.ppermute(value, AXES, pairs)  42.1 us
    ppermute x26, waiting for transfers between devices, swap(): return lax.ppermute(value, AXES, pairs)  38.7 us
    pallas_call x2, Pallas kernels, chol(): pl.pallas_call(kernel, in_specs=[VMEM, VMEM], out_specs=[VMEM, VMEM], out...  24.5 us
    pallas_call x1, Pallas kernels, finish(): pl.pallas_call(finish_kernel, in_specs=[hbm] + [VMEM] * 12, out_specs=hbm...  19.3 us
    ppermute x4, starting transfers between devices, scatter(): return lax.ppermute(value, AXES, pairs)  14.9 us
    ppermute x4, waiting for transfers between devices, scatter(): return lax.ppermute(value, AXES, pairs)  3.94 us
  transfers between devices with their start and end apart: 30, of which 11 were waited for; matrix products, arithmetic and copies ran while one was open for 3% of the time, Pallas kernels for 17%

profile of v1, /device:TPU:0, one launch (start us, length us, event | category | flops | bytes accessed | tf_op | source)
XLA Modules:
  0.0 156.3 jit_solution(4445436630408435071)
XLA Ops:
  0.0 2.7 %extract.1 = (f32[3,128,128]{2,1,0:T(8,128)}, f32[4,256,256]{2,1,0:T(8,128)}, f32[256,256]{1,0:T(8,128)}, f32[256,256]{1,0:T(8,128)}, f32[256,256]{1,0:T(8,128)}, /*index=5*/f32[256,256]{1,0:T(8,128)}) custom-call(f32[16384,128]{1,0:T(8,128)} %bitcast.10), custom_call_target="tpu_custom_call" | custom-call | tf_op jit(solution)/shard_map/extract/pallas_call | solution.py:89
  2.7 5.2 %collective-permute-start.18 = (f32[3,128,128]{2,1,0:T(8,128)}, f32[3,128,128]{2,1,0:T(8,128)S(1)}, u32[]{:S(2)}, u32[]{:S(2)}) collective-permute-start(f32[3,128,128]{2,1,0:T(8,128)} %get-tuple-element.30), channel_id=1, source_target_pairs={{0,64},{1,65},{16,80},{17,81}} | collective-permute-start | bytes 589832 | tf_op jit(solution)/shard_map/ppermute | solution.py:40
  10.6 2.9 %collective-permute-done.18 = f32[3,128,128]{2,1,0:T(8,128)S(1)} collective-permute-done((f32[3,128,128]{2,1,0:T(8,128)}, f32[3,128,128]{2,1,0:T(8,128)S(1)}, u32[]{:S(2)}, u32[]{:S(2)}) %collective-permute-start.18) | collective-permute-done | bytes 196640 | tf_op jit(solution)/shard_map/ppermute | solution.py:40
  13.7 2.9 %collective-permute-done.16 = f32[3,128,128]{2,1,0:T(8,128)S(1)} collective-permute-done((f32[3,128,128]{2,1,0:T(8,128)}, f32[3,128,128]{2,1,0:T(8,128)S(1)}, u32[]{:S(2)}, u32[]{:S(2)}) %collective-permute-start.16) | collective-permute-done | bytes 196640 | tf_op jit(solution)/shard_map/ppermute | solution.py:40
  17.5 1.3 collective-permute-start.21
  18.9 1.3 collective-permute-start.20
  20.2 1.3 collective-permute-start.19
  21.5 1.6 %collective-permute-start = (f32[256,256]{1,0:T(8,128)}, f32[256,256]{1,0:T(8,128)S(1)}, u32[]{:S(2)}, u32[]{:S(2)}) collective-permute-start(f32[256,256]{1,0:T(8,128)} %get-tuple-element.23), channel_id=1, source_target_pairs={{0,0},{1,17},{2,34},{3,51},{4,64},{5,81},{6,98},{7,115},{8,8},{9,2... | collective-permute-start | bytes 786440 | tf_op jit(solution)/shard_map/ppermute | solution.py:52
  23.1 3.1 %collective-permute-start.1 = (f32[256,256]{1,0:T(8,128)}, f32[256,256]{1,0:T(8,128)S(1)}, u32[]{:S(2)}, u32[]{:S(2)}) collective-permute-start(f32[256,256]{1,0:T(8,128)} %get-tuple-element.24), channel_id=1, source_target_pairs={{0,1},{1,16},{2,35},{3,50},{4,65},{5,80},{6,99},{7,114},{8,9},{9,2... | collective-permute-start | bytes 786440 | tf_op jit(solution)/shard_map/ppermute | solution.py:52
  26.3 1.3 collective-permute-start.2
  27.6 8.9 %collective-permute-start.3 = (f32[256,256]{1,0:T(8,128)}, f32[256,256]{1,0:T(8,128)S(1)}, u32[]{:S(2)}, u32[]{:S(2)}) collective-permute-start(f32[256,256]{1,0:T(8,128)} %get-tuple-element.26), channel_id=1, source_target_pairs={{0,3},{1,18},{2,33},{3,48},{4,67},{5,82},{6,97},{7,112},{8,11},{9,... | collective-permute-start | bytes 786440 | tf_op jit(solution)/shard_map/ppermute | solution.py:52
  36.5 1.9 %collective-permute-start.27 = (f32[3,128,128]{2,1,0:T(8,128)S(1)}, f32[3,128,128]{2,1,0:T(8,128)S(1)}, u32[]{:S(2)}, u32[]{:S(2)}) collective-permute-start(f32[3,128,128]{2,1,0:T(8,128)S(1)} %add_select_fusion.1), channel_id=1, source_target_pairs={{0,3},{1,2},{4,7},{5,6},{8,11},{9,10},{12,15},{13,14},{16,19},{17,... | collective-permute-start | bytes 589832 | tf_op jit(solution)/shard_map/ppermute | solution.py:40
  39.8 2.8 %collective-permute-start.25 = (f32[3,128,128]{2,1,0:T(8,128)S(1)}, f32[3,128,128]{2,1,0:T(8,128)S(1)}, u32[]{:S(2)}, u32[]{:S(2)}) collective-permute-start(f32[3,128,128]{2,1,0:T(8,128)S(1)} %add_select_fusion.1), channel_id=1, source_target_pairs={{0,1},{1,0},{4,5},{5,4},{8,9},{9,8},{12,13},{13,12},{16,17},{17,16... | collective-permute-start | bytes 589832 | tf_op jit(solution)/shard_map/ppermute | solution.py:40
  42.6 3.9 %collective-permute-done.3.s3 = f32[256,256]{1,0:T(8,128)S(1)} collective-permute-done((f32[256,256]{1,0:T(8,128)}, f32[256,256]{1,0:T(8,128)S(1)}, u32[]{:S(2)}, u32[]{:S(2)}) %collective-permute-start.3) | collective-permute-done | bytes 262176 | tf_op jit(solution)/shard_map/ppermute | solution.py:52
  47.3 2.0 %prep.1 = (f32[128,256]{1,0:T(8,128)}, f32[128,256]{1,0:T(8,128)}) custom-call(f32[256,256]{1,0:T(8,128)} %copy-done.7, f32[256,256]{1,0:T(8,128)} %copy-done.8, f32[256,256]{1,0:T(8,128)} %copy-done.9, f32[256,256]{1,0:T(8,128)} %copy-done.10), custom_call_target="tpu_custom_call" | custom-call | tf_op jit(solution)/shard_map/prep/pallas_call | solution.py:108
  50.0 3.4 %collective-permute-start.10 = (f32[128,256]{1,0:T(8,128)}, f32[128,256]{1,0:T(8,128)S(1)}, u32[]{:S(2)}, u32[]{:S(2)}) collective-permute-start(f32[128,256]{1,0:T(8,128)} %get-tuple-element.28), channel_id=1, source_target_pairs={{0,4},{1,5},{2,6},{3,7},{4,0},{5,1},{6,2},{7,3},{8,12},{9,13},{10,... | collective-permute-start | bytes 393224 | tf_op jit(solution)/shard_map/ppermute | solution.py:40
  53.6 3.7 %collective-permute-start.6 = (f32[128,256]{1,0:T(8,128)}, f32[128,256]{1,0:T(8,128)S(1)}, u32[]{:S(2)}, u32[]{:S(2)}) collective-permute-start(f32[128,256]{1,0:T(8,128)} %get-tuple-element.27), channel_id=1, source_target_pairs={{0,3},{1,2},{2,1},{3,0},{4,7},{5,6},{6,5},{7,4},{8,11},{9,10},{10,... | collective-permute-start | bytes 393224 | tf_op jit(solution)/shard_map/ppermute | solution.py:40
  57.3 4.2 %collective-permute-start.4 = (f32[128,256]{1,0:T(8,128)}, f32[128,256]{1,0:T(8,128)S(1)}, u32[]{:S(2)}, u32[]{:S(2)}) collective-permute-start(f32[128,256]{1,0:T(8,128)} %get-tuple-element.27), channel_id=1, source_target_pairs={{0,1},{1,0},{2,3},{3,2},{4,5},{5,4},{6,7},{7,6},{8,9},{9,8},{10,11... | collective-permute-start | bytes 393224 | tf_op jit(solution)/shard_map/ppermute | solution.py:40
  62.6 2.1 %collective-permute-start.14 = (f32[4,128,256]{2,1,0:T(8,128)S(1)}, f32[4,128,256]{2,1,0:T(8,128)}, u32[]{:S(2)}, u32[]{:S(2)}) collective-permute-start(f32[4,128,256]{2,1,0:T(8,128)S(1)} %pad_maximum_fusion.1.be0), channel_id=1, source_target_pairs={{0,2},{1,3},{2,0},{3,1},{4,6},{5,7},{6,4},{7,5},{8,10},{9,11},{10,... | collective-permute-start | bytes 1572872 | tf_op jit(solution)/shard_map/ppermute | solution.py:40
  67.1 1.5 collective-permute-start.24
  68.6 2.3 %collective-permute-start.23 = (f32[4,256,256]{2,1,0:T(8,128)}, f32[4,256,256]{2,1,0:T(8,128)}, u32[]{:S(2)}, u32[]{:S(2)}) collective-permute-start(f32[4,256,256]{2,1,0:T(8,128)} %get-tuple-element.31), channel_id=1, source_target_pairs={{0,64},{1,65},{2,66},{3,67},{4,68},{5,69},{6,70},{7,71},{8,72},{9,... | collective-permute-start | bytes 3145736 | tf_op jit(solution)/shard_map/ppermute | solution.py:40
  71.6 2.3 %collective-permute-start.22 = (f32[4,256,256]{2,1,0:T(8,128)}, f32[4,256,256]{2,1,0:T(8,128)}, u32[]{:S(2)}, u32[]{:S(2)}) collective-permute-start(f32[4,256,256]{2,1,0:T(8,128)} %get-tuple-element.31), channel_id=1, source_target_pairs={{0,32},{1,33},{2,34},{3,35},{4,36},{5,37},{6,38},{7,39},{8,40},{9,... | collective-permute-start | bytes 3145736 | tf_op jit(solution)/shard_map/ppermute | solution.py:40
  73.8 12.1 %shard_map.17 = (f32[4,4,128,128]{3,2,1,0:T(8,128)}, f32[4,4,128,128]{3,2,1,0:T(8,128)}) custom-call(f32[5,128,128]{2,1,0:T(8,128)} %copy-done.6, f32[5,128,128]{2,1,0:T(8,128)} %copy-done.11), custom_call_target="tpu_custom_call" | custom-call | flops 12000000000 | tf_op jit(solution)/shard_map/pallas_call | solution.py:244
  85.9 3.5 %collective-permute-done.24 = f32[4,256,256]{2,1,0:T(8,128)S(1)} collective-permute-done((f32[4,256,256]{2,1,0:T(8,128)}, f32[4,256,256]{2,1,0:T(8,128)S(1)}, u32[]{:S(2)}, u32[]{:S(2)}) %collective-permute-start.24) | collective-permute-done | bytes 1048608 | tf_op jit(solution)/shard_map/ppermute | solution.py:40
  89.4 2.4 %collective-permute-start.13 = (f32[4,128,256]{2,1,0:T(8,128)S(1)}, f32[4,128,256]{2,1,0:T(8,128)}, u32[]{:S(2)}, u32[]{:S(2)}) collective-permute-start(f32[4,128,256]{2,1,0:T(8,128)S(1)} %pad_maximum_fusion.1.be0), channel_id=1, source_target_pairs={{0,1},{1,0},{2,3},{3,2},{4,5},{5,4},{6,7},{7,6},{8,9},{9,8},{10,11... | collective-permute-start | bytes 1572872 | tf_op jit(solution)/shard_map/ppermute | solution.py:40
  91.8 2.0 %collective-permute-done.23 = f32[4,256,256]{2,1,0:T(8,128)} collective-permute-done((f32[4,256,256]{2,1,0:T(8,128)}, f32[4,256,256]{2,1,0:T(8,128)}, u32[]{:S(2)}, u32[]{:S(2)}) %collective-permute-start.23) | collective-permute-done | bytes 1048608 | tf_op jit(solution)/shard_map/ppermute | solution.py:40
  93.7 19.5 %collective-permute-done.22 = f32[4,256,256]{2,1,0:T(8,128)} collective-permute-done((f32[4,256,256]{2,1,0:T(8,128)}, f32[4,256,256]{2,1,0:T(8,128)}, u32[]{:S(2)}, u32[]{:S(2)}) %collective-permute-start.22) | collective-permute-done | bytes 1048608 | tf_op jit(solution)/shard_map/ppermute | solution.py:40
  113.2 1.4 collective-permute-start.8
  114.6 2.1 %add_select_fusion.mine_ref = f32[4,256,256]{2,1,0:T(8,128)S(1)} fusion(f32[4,256,256]{2,1,0:T(8,128)S(1)} %copy-done.4, f32[4,256,256]{2,1,0:T(8,128)} %copy-done.5, f32[4,256,256]{2,1,0:T(8,128)} %collective-permute-done.22, f32[4,256,256]{2,1,0:T(8,128)} %collective-permute-done.23, pred[]{:T(512)S(6)} %eq.28), kind=kLoop, calls=%fused_computation | loop fusion | flops 786432 | bytes 5242881 | tf_op jit(solution)/shard_map/jit(_where)/select_n | solution.py:457
  117.1 12.4 %shard_map.18 = (f32[4,4,128,128]{3,2,1,0:T(8,128)}, f32[4,4,128,128]{3,2,1,0:T(8,128)}) custom-call(f32[4,4,128,128]{3,2,1,0:T(8,128)} %get-tuple-element.37.s_in, f32[4,4,128,128]{3,2,1,0:T(8,128)} %get-tuple-element.38.inv_in), custom_call_target="tpu_custom_call" | custom-call | flops 12000000000 | tf_op jit(solution)/shard_map/pallas_call | solution.py:244
  129.6 6.2 %collective-permute-done.7.al1 = f32[4,128,256]{2,1,0:T(8,128)} collective-permute-done((f32[4,128,256]{2,1,0:T(8,128)S(1)}, f32[4,128,256]{2,1,0:T(8,128)}, u32[]{:S(2)}, u32[]{:S(2)}) %collective-permute-start.7) | collective-permute-done | bytes 524320 | tf_op jit(solution)/shard_map/ppermute | solution.py:40
  136.8 19.3 %finish.1 = f32[16384,128]{1,0:T(8,128)} custom-call(f32[16384,128]{1,0:T(8,128)} %bitcast.11, f32[4,128,256]{2,1,0:T(8,128)} %copy-done.2, f32[4,128,256]{2,1,0:T(8,128)} %collective-permute-done.7.al1, f32[4,128,256]{2,1,0:T(8,128)} %collective-permute-done.8.al2, f32[4,128,256]{2,1,0:T(8,128)} %collective-permute-done.9.al3, f32[4,128,256]{2,1,0:T(8,128)} %copy-done.1, ...), custom_call_target="tpu_custom_call" | custom-call | tf_op jit(solution)/shard_map/finish/pallas_call | solution.py:397
  (65 shorter events, 12.4 us)
Async XLA Ops:
  2.7 10.8 %collective-permute-start.18 = (f32[3,128,128]{2,1,0:T(8,128)}, f32[3,128,128]{2,1,0:T(8,128)S(1)}, u32[]{:S(2)}, u32[]{:S(2)}) collective-permute-start(f32[3,128,128]{2,1,0:T(8,128)} %get-tuple-element.30), channel_id=1, source_target_pairs={{0,64},{1,65},{16,80},{17,81}} | collective-permute-start | bytes 589832 | tf_op jit(solution)/shard_map/ppermute | solution.py:40
  7.9 5.7 %collective-permute-start.17 = (f32[3,128,128]{2,1,0:T(8,128)}, f32[3,128,128]{2,1,0:T(8,128)S(1)}, u32[]{:S(2)}, u32[]{:S(2)}) collective-permute-start(f32[3,128,128]{2,1,0:T(8,128)} %get-tuple-element.30), channel_id=1, source_target_pairs={{0,96},{1,97},{16,112},{17,113}} | collective-permute-start | bytes 589832 | tf_op jit(solution)/shard_map/ppermute | solution.py:40
  9.2 7.3 %collective-permute-start.16 = (f32[3,128,128]{2,1,0:T(8,128)}, f32[3,128,128]{2,1,0:T(8,128)S(1)}, u32[]{:S(2)}, u32[]{:S(2)}) collective-permute-start(f32[3,128,128]{2,1,0:T(8,128)} %get-tuple-element.30), channel_id=1, source_target_pairs={{0,32},{1,33},{16,48},{17,49}} | collective-permute-start | bytes 589832 | tf_op jit(solution)/shard_map/ppermute | solution.py:40
  17.5 8.7 %collective-permute-start.21 = (f32[3,128,128]{2,1,0:T(8,128)S(1)}, f32[3,128,128]{2,1,0:T(8,128)S(1)}, u32[]{:S(2)}, u32[]{:S(2)}) collective-permute-start(f32[3,128,128]{2,1,0:T(8,128)S(1)} %add_select_fusion.2), channel_id=1, source_target_pairs={{0,8},{1,9},{16,24},{17,25},{32,40},{33,41},{48,56},{49,57},{64,72... | collective-permute-start | bytes 589832 | tf_op jit(solution)/shard_map/ppermute | solution.py:40
  18.9 8.7 %collective-permute-start.20 = (f32[3,128,128]{2,1,0:T(8,128)S(1)}, f32[3,128,128]{2,1,0:T(8,128)S(1)}, u32[]{:S(2)}, u32[]{:S(2)}) collective-permute-start(f32[3,128,128]{2,1,0:T(8,128)S(1)} %add_select_fusion.2), channel_id=1, source_target_pairs={{0,12},{1,13},{16,28},{17,29},{32,44},{33,45},{48,60},{49,61},{64,... | collective-permute-start | bytes 589832 | tf_op jit(solution)/shard_map/ppermute | solution.py:40
  20.2 16.3 %collective-permute-start.19 = (f32[3,128,128]{2,1,0:T(8,128)S(1)}, f32[3,128,128]{2,1,0:T(8,128)S(1)}, u32[]{:S(2)}, u32[]{:S(2)}) collective-permute-start(f32[3,128,128]{2,1,0:T(8,128)S(1)} %add_select_fusion.2), channel_id=1, source_target_pairs={{0,4},{1,5},{16,20},{17,21},{32,36},{33,37},{48,52},{49,53},{64,68... | collective-permute-start | bytes 589832 | tf_op jit(solution)/shard_map/ppermute | solution.py:40
  21.5 17.0 %collective-permute-start = (f32[256,256]{1,0:T(8,128)}, f32[256,256]{1,0:T(8,128)S(1)}, u32[]{:S(2)}, u32[]{:S(2)}) collective-permute-start(f32[256,256]{1,0:T(8,128)} %get-tuple-element.23), channel_id=1, source_target_pairs={{0,0},{1,17},{2,34},{3,51},{4,64},{5,81},{6,98},{7,115},{8,8},{9,2... | collective-permute-start | bytes 786440 | tf_op jit(solution)/shard_map/ppermute | solution.py:52
  23.1 16.7 %collective-permute-start.1 = (f32[256,256]{1,0:T(8,128)}, f32[256,256]{1,0:T(8,128)S(1)}, u32[]{:S(2)}, u32[]{:S(2)}) collective-permute-start(f32[256,256]{1,0:T(8,128)} %get-tuple-element.24), channel_id=1, source_target_pairs={{0,1},{1,16},{2,35},{3,50},{4,65},{5,80},{6,99},{7,114},{8,9},{9,2... | collective-permute-start | bytes 786440 | tf_op jit(solution)/shard_map/ppermute | solution.py:52
  26.3 16.3 %collective-permute-start.2 = (f32[256,256]{1,0:T(8,128)}, f32[256,256]{1,0:T(8,128)S(1)}, u32[]{:S(2)}, u32[]{:S(2)}) collective-permute-start(f32[256,256]{1,0:T(8,128)} %get-tuple-element.25), channel_id=1, source_target_pairs={{0,2},{1,19},{2,32},{3,49},{4,66},{5,83},{6,96},{7,113},{8,10},{9,... | collective-permute-start | bytes 786440 | tf_op jit(solution)/shard_map/ppermute | solution.py:52
  27.6 19.0 %collective-permute-start.3 = (f32[256,256]{1,0:T(8,128)}, f32[256,256]{1,0:T(8,128)S(1)}, u32[]{:S(2)}, u32[]{:S(2)}) collective-permute-start(f32[256,256]{1,0:T(8,128)} %get-tuple-element.26), channel_id=1, source_target_pairs={{0,3},{1,18},{2,33},{3,48},{4,67},{5,82},{6,97},{7,112},{8,11},{9,... | collective-permute-start | bytes 786440 | tf_op jit(solution)/shard_map/ppermute | solution.py:52
  36.5 13.5 %collective-permute-start.27 = (f32[3,128,128]{2,1,0:T(8,128)S(1)}, f32[3,128,128]{2,1,0:T(8,128)S(1)}, u32[]{:S(2)}, u32[]{:S(2)}) collective-permute-start(f32[3,128,128]{2,1,0:T(8,128)S(1)} %add_select_fusion.1), channel_id=1, source_target_pairs={{0,3},{1,2},{4,7},{5,6},{8,11},{9,10},{12,15},{13,14},{16,19},{17,... | collective-permute-start | bytes 589832 | tf_op jit(solution)/shard_map/ppermute | solution.py:40
  38.5 14.9 %collective-permute-start.26 = (f32[3,128,128]{2,1,0:T(8,128)S(1)}, f32[3,128,128]{2,1,0:T(8,128)S(1)}, u32[]{:S(2)}, u32[]{:S(2)}) collective-permute-start(f32[3,128,128]{2,1,0:T(8,128)S(1)} %add_select_fusion.1), channel_id=1, source_target_pairs={{0,2},{1,3},{4,6},{5,7},{8,10},{9,11},{12,14},{13,15},{16,18},{17,... | collective-permute-start | bytes 589832 | tf_op jit(solution)/shard_map/ppermute | solution.py:40
  39.8 13.6 %collective-permute-start.25 = (f32[3,128,128]{2,1,0:T(8,128)S(1)}, f32[3,128,128]{2,1,0:T(8,128)S(1)}, u32[]{:S(2)}, u32[]{:S(2)}) collective-permute-start(f32[3,128,128]{2,1,0:T(8,128)S(1)} %add_select_fusion.1), channel_id=1, source_target_pairs={{0,1},{1,0},{4,5},{5,4},{8,9},{9,8},{12,13},{13,12},{16,17},{17,16... | collective-permute-start | bytes 589832 | tf_op jit(solution)/shard_map/ppermute | solution.py:40
  49.3 8.0 %collective-permute-start.12 = (f32[128,256]{1,0:T(8,128)}, f32[128,256]{1,0:T(8,128)S(1)}, u32[]{:S(2)}, u32[]{:S(2)}) collective-permute-start(f32[128,256]{1,0:T(8,128)} %get-tuple-element.28), channel_id=1, source_target_pairs={{0,12},{1,13},{2,14},{3,15},{4,8},{5,9},{6,10},{7,11},{8,4},{9,5},... | collective-permute-start | bytes 393224 | tf_op jit(solution)/shard_map/ppermute | solution.py:40
  49.3 8.0 %collective-permute-start.11 = (f32[128,256]{1,0:T(8,128)}, f32[128,256]{1,0:T(8,128)S(1)}, u32[]{:S(2)}, u32[]{:S(2)}) collective-permute-start(f32[128,256]{1,0:T(8,128)} %get-tuple-element.28), channel_id=1, source_target_pairs={{0,8},{1,9},{2,10},{3,11},{4,12},{5,13},{6,14},{7,15},{8,0},{9,1},... | collective-permute-start | bytes 393224 | tf_op jit(solution)/shard_map/ppermute | solution.py:40
  50.0 11.5 %collective-permute-start.10 = (f32[128,256]{1,0:T(8,128)}, f32[128,256]{1,0:T(8,128)S(1)}, u32[]{:S(2)}, u32[]{:S(2)}) collective-permute-start(f32[128,256]{1,0:T(8,128)} %get-tuple-element.28), channel_id=1, source_target_pairs={{0,4},{1,5},{2,6},{3,7},{4,0},{5,1},{6,2},{7,3},{8,12},{9,13},{10,... | collective-permute-start | bytes 393224 | tf_op jit(solution)/shard_map/ppermute | solution.py:40
  53.5 17.4 %collective-permute-start.28 = (f32[5,128,128]{2,1,0:T(8,128)S(1)}, f32[5,128,128]{2,1,0:T(8,128)S(1)}, u32[]{:S(2)}, u32[]{:S(2)}) collective-permute-start(f32[5,128,128]{2,1,0:T(8,128)S(1)} %pad_maximum_fusion.2.mine_ref), channel_id=1, source_target_pairs={{0,16},{1,17},{2,18},{3,19},{4,20},{5,21},{6,22},{7,23},{8,24},{9,... | collective-permute-start | bytes 983048 | tf_op jit(solution)/shard_map/ppermute | solution.py:40
  53.6 9.0 %collective-permute-start.6 = (f32[128,256]{1,0:T(8,128)}, f32[128,256]{1,0:T(8,128)S(1)}, u32[]{:S(2)}, u32[]{:S(2)}) collective-permute-start(f32[128,256]{1,0:T(8,128)} %get-tuple-element.27), channel_id=1, source_target_pairs={{0,3},{1,2},{2,1},{3,0},{4,7},{5,6},{6,5},{7,4},{8,11},{9,10},{10,... | collective-permute-start | bytes 393224 | tf_op jit(solution)/shard_map/ppermute | solution.py:40
  57.3 8.1 %collective-permute-start.5 = (f32[128,256]{1,0:T(8,128)}, f32[128,256]{1,0:T(8,128)S(1)}, u32[]{:S(2)}, u32[]{:S(2)}) collective-permute-start(f32[128,256]{1,0:T(8,128)} %get-tuple-element.27), channel_id=1, source_target_pairs={{0,2},{1,3},{2,0},{3,1},{4,6},{5,7},{6,4},{7,5},{8,10},{9,11},{10,... | collective-permute-start | bytes 393224 | tf_op jit(solution)/shard_map/ppermute | solution.py:40
  57.3 8.8 %collective-permute-start.4 = (f32[128,256]{1,0:T(8,128)}, f32[128,256]{1,0:T(8,128)S(1)}, u32[]{:S(2)}, u32[]{:S(2)}) collective-permute-start(f32[128,256]{1,0:T(8,128)} %get-tuple-element.27), channel_id=1, source_target_pairs={{0,1},{1,0},{2,3},{3,2},{4,5},{5,4},{6,7},{7,6},{8,9},{9,8},{10,11... | collective-permute-start | bytes 393224 | tf_op jit(solution)/shard_map/ppermute | solution.py:40
  62.5 54.2 %collective-permute-start.15 = (f32[4,128,256]{2,1,0:T(8,128)S(1)}, f32[4,128,256]{2,1,0:T(8,128)}, u32[]{:S(2)}, u32[]{:S(2)}) collective-permute-start(f32[4,128,256]{2,1,0:T(8,128)S(1)} %pad_maximum_fusion.1.be0), channel_id=1, source_target_pairs={{0,3},{1,2},{2,1},{3,0},{4,7},{5,6},{6,5},{7,4},{8,11},{9,10},{10,... | collective-permute-start | bytes 1572872 | tf_op jit(solution)/shard_map/ppermute | solution.py:40
  62.6 54.2 %collective-permute-start.14 = (f32[4,128,256]{2,1,0:T(8,128)S(1)}, f32[4,128,256]{2,1,0:T(8,128)}, u32[]{:S(2)}, u32[]{:S(2)}) collective-permute-start(f32[4,128,256]{2,1,0:T(8,128)S(1)} %pad_maximum_fusion.1.be0), channel_id=1, source_target_pairs={{0,2},{1,3},{2,0},{3,1},{4,6},{5,7},{6,4},{7,5},{8,10},{9,11},{10,... | collective-permute-start | bytes 1572872 | tf_op jit(solution)/shard_map/ppermute | solution.py:40
  67.1 49.7 %copy-start.2 = (f32[4,128,256]{2,1,0:T(8,128)}, f32[4,128,256]{2,1,0:T(8,128)S(1)}, u32[]{:S(2)}) copy-start(f32[4,128,256]{2,1,0:T(8,128)S(1)} %pad_maximum_fusion.al0) | copy-start | bytes 1572868
  67.1 47.5 %copy-start.4 = (f32[4,256,256]{2,1,0:T(8,128)S(1)}, f32[4,256,256]{2,1,0:T(8,128)}, u32[]{:S(2)}) copy-start(f32[4,256,256]{2,1,0:T(8,128)} %get-tuple-element.31) | copy-start | bytes 3145732
  67.1 22.3 %collective-permute-start.24 = (f32[4,256,256]{2,1,0:T(8,128)}, f32[4,256,256]{2,1,0:T(8,128)S(1)}, u32[]{:S(2)}, u32[]{:S(2)}) collective-permute-start(f32[4,256,256]{2,1,0:T(8,128)} %get-tuple-element.31), channel_id=1, source_target_pairs={{0,96},{1,97},{2,98},{3,99},{4,100},{5,101},{6,102},{7,103},{8,104... | collective-permute-start | bytes 3145736 | tf_op jit(solution)/shard_map/ppermute | solution.py:40
  68.6 25.1 %collective-permute-start.23 = (f32[4,256,256]{2,1,0:T(8,128)}, f32[4,256,256]{2,1,0:T(8,128)}, u32[]{:S(2)}, u32[]{:S(2)}) collective-permute-start(f32[4,256,256]{2,1,0:T(8,128)} %get-tuple-element.31), channel_id=1, source_target_pairs={{0,64},{1,65},{2,66},{3,67},{4,68},{5,69},{6,70},{7,71},{8,72},{9,... | collective-permute-start | bytes 3145736 | tf_op jit(solution)/shard_map/ppermute | solution.py:40
  71.6 41.6 %collective-permute-start.22 = (f32[4,256,256]{2,1,0:T(8,128)}, f32[4,256,256]{2,1,0:T(8,128)}, u32[]{:S(2)}, u32[]{:S(2)}) collective-permute-start(f32[4,256,256]{2,1,0:T(8,128)} %get-tuple-element.31), channel_id=1, source_target_pairs={{0,32},{1,33},{2,34},{3,35},{4,36},{5,37},{6,38},{7,39},{8,40},{9,... | collective-permute-start | bytes 3145736 | tf_op jit(solution)/shard_map/ppermute | solution.py:40
  89.4 40.2 %collective-permute-start.13 = (f32[4,128,256]{2,1,0:T(8,128)S(1)}, f32[4,128,256]{2,1,0:T(8,128)}, u32[]{:S(2)}, u32[]{:S(2)}) collective-permute-start(f32[4,128,256]{2,1,0:T(8,128)S(1)} %pad_maximum_fusion.1.be0), channel_id=1, source_target_pairs={{0,1},{1,0},{2,3},{3,2},{4,5},{5,4},{6,7},{7,6},{8,9},{9,8},{10,11... | collective-permute-start | bytes 1572872 | tf_op jit(solution)/shard_map/ppermute | solution.py:40
  93.7 35.8 %collective-permute-start.9 = (f32[4,128,256]{2,1,0:T(8,128)S(1)}, f32[4,128,256]{2,1,0:T(8,128)}, u32[]{:S(2)}, u32[]{:S(2)}) collective-permute-start(f32[4,128,256]{2,1,0:T(8,128)S(1)} %pad_maximum_fusion.al0), channel_id=1, source_target_pairs={{0,12},{1,13},{2,14},{3,15},{4,8},{5,9},{6,10},{7,11},{8,4},{9,5},... | collective-permute-start | bytes 1572872 | tf_op jit(solution)/shard_map/ppermute | solution.py:40
  113.2 16.4 %collective-permute-start.8 = (f32[4,128,256]{2,1,0:T(8,128)S(1)}, f32[4,128,256]{2,1,0:T(8,128)}, u32[]{:S(2)}, u32[]{:S(2)}) collective-permute-start(f32[4,128,256]{2,1,0:T(8,128)S(1)} %pad_maximum_fusion.al0), channel_id=1, source_target_pairs={{0,8},{1,9},{2,10},{3,11},{4,12},{5,13},{6,14},{7,15},{8,0},{9,1},... | collective-permute-start | bytes 1572872 | tf_op jit(solution)/shard_map/ppermute | solution.py:40
  116.7 19.1 %collective-permute-start.7 = (f32[4,128,256]{2,1,0:T(8,128)S(1)}, f32[4,128,256]{2,1,0:T(8,128)}, u32[]{:S(2)}, u32[]{:S(2)}) collective-permute-start(f32[4,128,256]{2,1,0:T(8,128)S(1)} %pad_maximum_fusion.al0), channel_id=1, source_target_pairs={{0,4},{1,5},{2,6},{3,7},{4,0},{5,1},{6,2},{7,3},{8,12},{9,13},{10,... | collective-permute-start | bytes 1572872 | tf_op jit(solution)/shard_map/ppermute | solution.py:40
  116.8 19.0 %collective-permute-start.29 = (f32[4,256,256]{2,1,0:T(8,128)S(1)}, f32[4,256,256]{2,1,0:T(8,128)S(1)}, u32[]{:S(2)}, u32[]{:S(2)}) collective-permute-start(f32[4,256,256]{2,1,0:T(8,128)S(1)} %add_select_fusion.mine_ref), channel_id=1, source_target_pairs={{0,16},{1,17},{2,18},{3,19},{4,20},{5,21},{6,22},{7,23},{8,24},{9,... | collective-permute-start | bytes 3145736 | tf_op jit(solution)/shard_map/ppermute | solution.py:40
  (10 other events, 106.5 us)

commit v2 on v1

--- a/solution.py
+++ b/solution.py
@@ -66,7 +66,11 @@
     return hi, lo
 
 
-def extract_kernel(a_ref, corner_ref, whole_ref, *part_refs):
+def extract_kernel(a_hbm, corner_ref, whole_ref, p0_ref, p1_ref, p2_ref, p3_ref, a_ref, sem):
+    part_refs = (p0_ref, p1_ref, p2_ref, p3_ref)
+    copy = pltpu.make_async_copy(a_hbm.at[pl.ds(0, NB * 8)], a_ref, sem)
+    copy.start()
+    copy.wait()
     k = lax.axis_index("row") % NK
     x = lax.axis_index("col") % NX
 
@@ -88,10 +92,11 @@
     shapes = [(3, HALF, HALF), (4, NB, NB)] + [(NB, NB)] * 4
     return pl.pallas_call(
         extract_kernel,
-        grid=(1,),
-        in_specs=[pl.BlockSpec((NB * 8, HALF), lambda i: (0, 0))],
+        in_specs=[pl.BlockSpec(memory_space=pltpu.HBM)],
         out_specs=[VMEM] * 6,
+        scratch_shapes=[pltpu.VMEM((NB * 8, HALF), F32), pltpu.SemaphoreType.DMA],
         out_shape=[jax.ShapeDtypeStruct(shape, F32) for shape in shapes],
+        compiler_params=pltpu.CompilerParams(vmem_limit_bytes=57 * 1024 * 1024),
         name="extract",
     )(view)
 
@@ -105,24 +110,29 @@
 
 def prep(parts):
     half = jax.ShapeDtypeStruct((HALF, NB), F32)
-    return pl.pallas_call(prep_kernel, out_shape=(half, half), name="prep")(*parts)
+    return pl.pallas_call(
+        prep_kernel,
+        out_shape=(half, half),
+        compiler_params=pltpu.CompilerParams(vmem_limit_bytes=4 * 1024 * 1024),
+        name="prep",
+    )(*parts)
 
 
 def factor_diagonal(a_ref, m_ref, u_ref, t_ref):
     rows = lax.broadcasted_iota(jnp.int32, (HALF, HALF), 0)
     cols = lax.broadcasted_iota(jnp.int32, (HALF, HALF), 1)
-    m_ref[...] = jnp.where(rows == cols, 1.0, 0.0).astype(F32)
+    m_ref[:HALF] = jnp.where(rows == cols, 1.0, 0.0).astype(F32)
     full = (GROUP, HALF)
     groups = HALF // GROUP
     for step in range(groups):
         base = step * GROUP
         pivot = a_ref[base:base + GROUP, :]
         for k in range(GROUP):
-            t_ref[k] = jnp.broadcast_to(pivot[:, base + k:base + k + 1], full)
+            t_ref[k, :GROUP] = jnp.broadcast_to(pivot[:, base + k:base + k + 1], full)
         s = [[None] * GROUP for _ in range(GROUP)]
         for i in range(GROUP):
             for k in range(i + 1):
-                s[i][k] = jnp.broadcast_to(t_ref[k, i:i + 1, :], full)
+                s[i][k] = t_ref[k, pl.ds(i, GROUP, stride=0), :]
         low = [[None] * GROUP for _ in range(GROUP)]
         inv_d = [None] * GROUP
         root = [None] * GROUP
@@ -143,7 +153,7 @@
                 inv[i][j] = -total
         weights = []
         for ref, out in ((a_ref, u_ref), (m_ref, m_ref)):
-            raw = [jnp.broadcast_to(ref[base + i:base + i + 1, :], full) for i in range(GROUP)]
+            raw = [ref[pl.ds(base + i, GROUP, stride=0), :] for i in range(GROUP)]
             z = []
             for i in range(GROUP):
                 total = raw[i]
@@ -183,9 +193,9 @@
     zero = jnp.zeros((HALF, HALF), F32)
 
     def body(p, carry):
-        a_ref[...] = s_ref[p, p]
+        a_ref[:HALF] = s_ref[p, p]
         factor_diagonal(a_ref, m_ref, u_ref, t_ref)
-        inverse = m_ref[...]
+        inverse = m_ref[:HALF]
         s_ref[p, p] = jnp.where(lower, u_ref[...].T, 0.0)
         for q in range(first, last):
 
@@ -248,11 +258,12 @@
         out_shape=(tiles, tiles),
         cost_estimate=pl.CostEstimate(flops=flops, bytes_accessed=0, transcendentals=0),
         scratch_shapes=[
+            pltpu.VMEM((HALF + GROUP, HALF), F32),
+            pltpu.VMEM((HALF + GROUP, HALF), F32),
             pltpu.VMEM((HALF, HALF), F32),
-            pltpu.VMEM((HALF, HALF), F32),
-            pltpu.VMEM((HALF, HALF), F32),
-            pltpu.VMEM((GROUP, GROUP, HALF), F32),
+            pltpu.VMEM((GROUP, 2 * GROUP, HALF), F32),
         ],
+        compiler_params=pltpu.CompilerParams(vmem_limit_bytes=8 * 1024 * 1024),
     )(*operands)
 
 
@@ -272,8 +283,8 @@
 
 
 def finish_kernel(
-    a_hbm, al0, al1, al2, al3, be0, be1, be2, be3, mine_ref, other_ref, l_ref, inv_ref,
-    out_hbm, buf, lh_ref, c_ref, p_ref, pk_ref, sem_in, sem_out,
+    a_ref, al0, al1, al2, al3, be0, be1, be2, be3, mine_ref, other_ref, l_ref, inv_ref,
+    out_hbm, buf, lh_ref, c_ref, p_ref, pk_ref, sem_out,
 ):
     row = lax.axis_index("row")
     col = lax.axis_index("col")
@@ -287,14 +298,8 @@
         pair, ex = t // 4, t % 4
         return ((z // 2) ^ pair) + 2 * ((x ^ ex) ^ (row % 4))
 
-    def load(t):
-        return pltpu.make_async_copy(a_hbm.at[pl.ds(block_of(t) * size, size)], buf.at[t], sem_in.at[t])
-
     def store(t):
         return pltpu.make_async_copy(buf.at[t], out_hbm.at[pl.ds(block_of(t) * size, size)], sem_out.at[t])
-
-    for t in range(8):
-        load(t).start()
 
     for i in range(4):
         for j in range(4):
@@ -350,8 +355,6 @@
         )
 
     def step(u, carry):
-        for m in range(2):
-            load(2 * u + m).wait()
         left = pk_ref[pl.ds(2 * u, 2)].reshape(2 * NB, 3 * W)
         for b in range(4):
             update = jnp.dot(left, c_ref[:, b * NB:(b + 1) * NB], preferred_element_type=F32)
@@ -359,7 +362,8 @@
                 for h in range(2):
                     rows = pl.ds(2 * b + h, NB, stride=8)
                     part = update[m * NB:(m + 1) * NB, h * HALF:(h + 1) * HALF]
-                    buf[2 * u + m, rows, :] = buf[2 * u + m, rows, :] - part
+                    source = pl.ds(block_of(2 * u + m) * size + 2 * b + h, NB, stride=8)
+                    buf[2 * u + m, rows, :] = a_ref[source, :] - part
 
         for m in range(2):
             t = 2 * u + m
@@ -396,7 +400,7 @@
     hbm = pl.BlockSpec(memory_space=pl.ANY)
     return pl.pallas_call(
         finish_kernel,
-        in_specs=[hbm] + [VMEM] * 12,
+        in_specs=[VMEM] * 13,
         out_specs=hbm,
         out_shape=jax.ShapeDtypeStruct(view.shape, F32),
         scratch_shapes=[
@@ -406,9 +410,8 @@
             pltpu.VMEM((8, NB, W), F32),
             pltpu.VMEM((8, NB, 3 * W), BF16),
             pltpu.SemaphoreType.DMA((8,)),
-            pltpu.SemaphoreType.DMA((8,)),
         ],
-        compiler_params=pltpu.CompilerParams(vmem_limit_bytes=56 * 1024 * 1024),
+        compiler_params=pltpu.CompilerParams(vmem_limit_bytes=28 * 1024 * 1024),
         name="finish",
     )(view, *alphas, *betas, mine, other, lower, inverse)
 

time: 159 us -> 151 us (0.950)
  waiting for transfers between devices: 42.6 us -> 58.5 us
  Pallas kernels: 48.5 us -> 37.8 us
  starting transfers between devices: 57 us -> 50.4 us
  other arithmetic: 5.11 us -> 1.45 us
  local copies, waits for them, and re-layouts: 2.46 us -> 0.02 us
    ppermute x26, waiting for transfers between devices: 38.7 us -> 54.6 us  [swap(): return lax.ppermute(value, AXES, pairs)]
    ppermute x26, starting transfers between devices: 42.1 us -> 35.5 us  [swap(): return lax.ppermute(value, AXES, pairs)]
    pallas_call x3, Pallas kernels: 24.1 us -> 18.6 us  [the longest x1 15.8 us: finish(): pl.pallas_call(finish_kernel, in_specs=[VMEM] * 13, out_specs=hbm, out_sh...]
    pallas_call x2, Pallas kernels: 24.5 us -> 19.1 us  [chol(): pl.pallas_call(kernel, in_specs=[VMEM, VMEM], out_specs=[VMEM, VMEM], out...]
    unnamed x24 -> x6, local copies, waits for them, and re-layouts: 2.46 us -> 0.02 us
    select_n x1, other arithmetic: 2.13 us -> 0.27 us  [local(): mine = jnp.where(y == 0, blocks, got[0] + got[1] + got[2])]
  transfers between devices with their start and end apart: 30 -> 30, of which waited for: 11 -> 13; matrix products, arithmetic and copies ran while one was open for 3% -> 0% of each run, Pallas kernels for 17% -> 13%
where the time goes in v2:
time: 151 us; the launch traced here: 149 us
  waiting for transfers between devices  58.5 us (39%)
  starting transfers between devices  50.4 us (33%)
  Pallas kernels  37.8 us (25%)
    ppermute x26, waiting for transfers between devices, swap(): return lax.ppermute(value, AXES, pairs)  54.6 us
    ppermute x26, starting transfers between devices, swap(): return lax.ppermute(value, AXES, pairs)  35.5 us
    pallas_call x2, Pallas kernels, chol(): pl.pallas_call(kernel, in_specs=[VMEM, VMEM], out_specs=[VMEM, VMEM], out...  19.1 us
    pallas_call x1, Pallas kernels, finish(): pl.pallas_call(finish_kernel, in_specs=[VMEM] * 13, out_specs=hbm, out_sh...  15.8 us
    ppermute x4, starting transfers between devices, scatter(): return lax.ppermute(value, AXES, pairs)  14.9 us
    ppermute x4, waiting for transfers between devices, scatter(): return lax.ppermute(value, AXES, pairs)  3.97 us
  transfers between devices with their start and end apart: 30, of which 13 were waited for; matrix products, arithmetic and copies ran while one was open for 0% of the time, Pallas kernels for 13%

profile of v2, /device:TPU:0, one launch (start us, length us, event | category | flops | bytes accessed | tf_op | source)
XLA Modules:
  0.0 148.7 jit_solution(1501041897292562408)
XLA Ops:
  0.0 2.7 %extract.1 = (f32[3,128,128]{2,1,0:T(8,128)}, f32[4,256,256]{2,1,0:T(8,128)}, f32[256,256]{1,0:T(8,128)}, f32[256,256]{1,0:T(8,128)}, f32[256,256]{1,0:T(8,128)}, /*index=5*/f32[256,256]{1,0:T(8,128)}) custom-call(f32[16384,128]{1,0:T(8,128)} %bitcast.10), custom_call_target="tpu_custom_call" | custom-call | tf_op jit(solution)/shard_map/extract/pallas_call | solution.py:93
  2.7 5.2 %collective-permute-start.18 = (f32[3,128,128]{2,1,0:T(8,128)}, f32[3,128,128]{2,1,0:T(8,128)S(1)}, u32[]{:S(2)}, u32[]{:S(2)}) collective-permute-start(f32[3,128,128]{2,1,0:T(8,128)} %get-tuple-element.30), channel_id=1, source_target_pairs={{0,64},{1,65},{16,80},{17,81}} | collective-permute-start | bytes 589832 | tf_op jit(solution)/shard_map/ppermute | solution.py:40
  10.6 2.9 %collective-permute-done.18 = f32[3,128,128]{2,1,0:T(8,128)S(1)} collective-permute-done((f32[3,128,128]{2,1,0:T(8,128)}, f32[3,128,128]{2,1,0:T(8,128)S(1)}, u32[]{:S(2)}, u32[]{:S(2)}) %collective-permute-start.18) | collective-permute-done | bytes 196640 | tf_op jit(solution)/shard_map/ppermute | solution.py:40
  13.7 2.9 %collective-permute-done.16 = f32[3,128,128]{2,1,0:T(8,128)S(1)} collective-permute-done((f32[3,128,128]{2,1,0:T(8,128)}, f32[3,128,128]{2,1,0:T(8,128)S(1)}, u32[]{:S(2)}, u32[]{:S(2)}) %collective-permute-start.16) | collective-permute-done | bytes 196640 | tf_op jit(solution)/shard_map/ppermute | solution.py:40
  17.6 1.3 collective-permute-start.21
  18.9 1.3 collective-permute-start.20
  20.2 1.3 collective-permute-start.19
  21.5 1.6 %collective-permute-start = (f32[256,256]{1,0:T(8,128)}, f32[256,256]{1,0:T(8,128)S(1)}, u32[]{:S(2)}, u32[]{:S(2)}) collective-permute-start(f32[256,256]{1,0:T(8,128)} %get-tuple-element.23), channel_id=1, source_target_pairs={{0,0},{1,17},{2,34},{3,51},{4,64},{5,81},{6,98},{7,115},{8,8},{9,2... | collective-permute-start | bytes 786440 | tf_op jit(solution)/shard_map/ppermute | solution.py:52
  23.1 3.1 %collective-permute-start.1 = (f32[256,256]{1,0:T(8,128)}, f32[256,256]{1,0:T(8,128)S(1)}, u32[]{:S(2)}, u32[]{:S(2)}) collective-permute-start(f32[256,256]{1,0:T(8,128)} %get-tuple-element.24), channel_id=1, source_target_pairs={{0,1},{1,16},{2,35},{3,50},{4,65},{5,80},{6,99},{7,114},{8,9},{9,2... | collective-permute-start | bytes 786440 | tf_op jit(solution)/shard_map/ppermute | solution.py:52
  26.3 1.3 collective-permute-start.2
  27.6 8.9 %collective-permute-start.3 = (f32[256,256]{1,0:T(8,128)}, f32[256,256]{1,0:T(8,128)S(1)}, u32[]{:S(2)}, u32[]{:S(2)}) collective-permute-start(f32[256,256]{1,0:T(8,128)} %get-tuple-element.26), channel_id=1, source_target_pairs={{0,3},{1,18},{2,33},{3,48},{4,67},{5,82},{6,97},{7,112},{8,11},{9,... | collective-permute-start | bytes 786440 | tf_op jit(solution)/shard_map/ppermute | solution.py:52
  36.5 1.9 %collective-permute-start.27 = (f32[3,128,128]{2,1,0:T(8,128)S(1)}, f32[3,128,128]{2,1,0:T(8,128)S(1)}, u32[]{:S(2)}, u32[]{:S(2)}) collective-permute-start(f32[3,128,128]{2,1,0:T(8,128)S(1)} %add_select_fusion.1), channel_id=1, source_target_pairs={{0,3},{1,2},{4,7},{5,6},{8,11},{9,10},{12,15},{13,14},{16,19},{17,... | collective-permute-start | bytes 589832 | tf_op jit(solution)/shard_map/ppermute | solution.py:40
  39.8 2.8 %collective-permute-start.25 = (f32[3,128,128]{2,1,0:T(8,128)S(1)}, f32[3,128,128]{2,1,0:T(8,128)S(1)}, u32[]{:S(2)}, u32[]{:S(2)}) collective-permute-start(f32[3,128,128]{2,1,0:T(8,128)S(1)} %add_select_fusion.1), channel_id=1, source_target_pairs={{0,1},{1,0},{4,5},{5,4},{8,9},{9,8},{12,13},{13,12},{16,17},{17,16... | collective-permute-start | bytes 589832 | tf_op jit(solution)/shard_map/ppermute | solution.py:40
  42.6 4.0 %collective-permute-done.3.s3 = f32[256,256]{1,0:T(8,128)S(1)} collective-permute-done((f32[256,256]{1,0:T(8,128)}, f32[256,256]{1,0:T(8,128)S(1)}, u32[]{:S(2)}, u32[]{:S(2)}) %collective-permute-start.3) | collective-permute-done | bytes 262176 | tf_op jit(solution)/shard_map/ppermute | solution.py:52
  46.9 2.5 %collective-permute-done.27 = f32[3,128,128]{2,1,0:T(8,128)S(1)} collective-permute-done((f32[3,128,128]{2,1,0:T(8,128)S(1)}, f32[3,128,128]{2,1,0:T(8,128)S(1)}, u32[]{:S(2)}, u32[]{:S(2)}) %collective-permute-start.27) | collective-permute-done | bytes 196640 | tf_op jit(solution)/shard_map/ppermute | solution.py:40
  49.4 1.4 collective-permute-start.10
  51.1 3.7 %collective-permute-start.6 = (f32[128,256]{1,0:T(8,128)S(1)}, f32[128,256]{1,0:T(8,128)S(1)}, u32[]{:S(2)}, u32[]{:S(2)}) collective-permute-start(f32[128,256]{1,0:T(8,128)S(1)} %get-tuple-element.27), channel_id=1, source_target_pairs={{0,3},{1,2},{2,1},{3,0},{4,7},{5,6},{6,5},{7,4},{8,11},{9,10},{10,... | collective-permute-start | bytes 393224 | tf_op jit(solution)/shard_map/ppermute | solution.py:40
  54.8 4.0 %collective-permute-start.4 = (f32[128,256]{1,0:T(8,128)S(1)}, f32[128,256]{1,0:T(8,128)S(1)}, u32[]{:S(2)}, u32[]{:S(2)}) collective-permute-start(f32[128,256]{1,0:T(8,128)S(1)} %get-tuple-element.27), channel_id=1, source_target_pairs={{0,1},{1,0},{2,3},{3,2},{4,5},{5,4},{6,7},{7,6},{8,9},{9,8},{10,11... | collective-permute-start | bytes 393224 | tf_op jit(solution)/shard_map/ppermute | solution.py:40
  59.0 2.2 %collective-permute-done.6 = f32[128,256]{1,0:T(8,128)S(1)} collective-permute-done((f32[128,256]{1,0:T(8,128)S(1)}, f32[128,256]{1,0:T(8,128)S(1)}, u32[]{:S(2)}, u32[]{:S(2)}) %collective-permute-start.6) | collective-permute-done | bytes 131104 | tf_op jit(solution)/shard_map/ppermute | solution.py:40
  61.1 1.5 collective-permute-done.5
  63.2 1.5 %collective-permute-start.24 = (f32[4,256,256]{2,1,0:T(8,128)}, f32[4,256,256]{2,1,0:T(8,128)S(1)}, u32[]{:S(2)}, u32[]{:S(2)}) collective-permute-start(f32[4,256,256]{2,1,0:T(8,128)} %get-tuple-element.31), channel_id=1, source_target_pairs={{0,96},{1,97},{2,98},{3,99},{4,100},{5,101},{6,102},{7,103},{8,104... | collective-permute-start | bytes 3145736 | tf_op jit(solution)/shard_map/ppermute | solution.py:40
  64.7 1.4 collective-permute-start.23
  66.1 1.4 collective-permute-start.22
  67.5 9.6 %shard_map.17 = (f32[4,4,128,128]{3,2,1,0:T(8,128)S(1)}, f32[4,4,128,128]{3,2,1,0:T(8,128)S(1)}) custom-call(f32[5,128,128]{2,1,0:T(8,128)S(1)} %pad_maximum_fusion.2.mine_ref, f32[5,128,128]{2,1,0:T(8,128)S(1)} %collective-permute-done.28.other_ref), custom_call_target="tpu_custom_call" | custom-call | flops 12000000000 | tf_op jit(solution)/shard_map/pallas_call | solution.py:254
  77.1 8.6 %collective-permute-done.24 = f32[4,256,256]{2,1,0:T(8,128)S(1)} collective-permute-done((f32[4,256,256]{2,1,0:T(8,128)}, f32[4,256,256]{2,1,0:T(8,128)S(1)}, u32[]{:S(2)}, u32[]{:S(2)}) %collective-permute-start.24) | collective-permute-done | bytes 1048608 | tf_op jit(solution)/shard_map/ppermute | solution.py:40
  85.7 2.4 %collective-permute-start.13 = (f32[4,128,256]{2,1,0:T(8,128)S(1)}, f32[4,128,256]{2,1,0:T(8,128)S(1)}, u32[]{:S(2)}, u32[]{:S(2)}) collective-permute-start(f32[4,128,256]{2,1,0:T(8,128)S(1)} %pad_maximum_fusion.1.be0), channel_id=1, source_target_pairs={{0,1},{1,0},{2,3},{3,2},{4,5},{5,4},{6,7},{7,6},{8,9},{9,8},{10,11... | collective-permute-start | bytes 1572872 | tf_op jit(solution)/shard_map/ppermute | solution.py:40
  88.1 1.8 %collective-permute-done.23 = f32[4,256,256]{2,1,0:T(8,128)S(1)} collective-permute-done((f32[4,256,256]{2,1,0:T(8,128)}, f32[4,256,256]{2,1,0:T(8,128)S(1)}, u32[]{:S(2)}, u32[]{:S(2)}) %collective-permute-start.23) | collective-permute-done | bytes 1048608 | tf_op jit(solution)/shard_map/ppermute | solution.py:40
  89.9 19.7 %collective-permute-done.22 = f32[4,256,256]{2,1,0:T(8,128)S(1)} collective-permute-done((f32[4,256,256]{2,1,0:T(8,128)}, f32[4,256,256]{2,1,0:T(8,128)S(1)}, u32[]{:S(2)}, u32[]{:S(2)}) %collective-permute-start.22) | collective-permute-done | bytes 1048608 | tf_op jit(solution)/shard_map/ppermute | solution.py:40
  111.5 9.5 %shard_map.18 = (f32[4,4,128,128]{3,2,1,0:T(8,128)S(1)}, f32[4,4,128,128]{3,2,1,0:T(8,128)S(1)}) custom-call(f32[4,4,128,128]{3,2,1,0:T(8,128)S(1)} %get-tuple-element.37.s_in, f32[4,4,128,128]{3,2,1,0:T(8,128)S(1)} %get-tuple-element.38.inv_in), custom_call_target="tpu_custom_call" | custom-call | flops 12000000000 | tf_op jit(solution)/shard_map/pallas_call | solution.py:254
  121.0 4.8 %collective-permute-done.8.al2 = f32[4,128,256]{2,1,0:T(8,128)S(1)} collective-permute-done((f32[4,128,256]{2,1,0:T(8,128)S(1)}, f32[4,128,256]{2,1,0:T(8,128)S(1)}, u32[]{:S(2)}, u32[]{:S(2)}) %collective-permute-start.8) | collective-permute-done | bytes 524320 | tf_op jit(solution)/shard_map/ppermute | solution.py:40
  125.9 6.9 %collective-permute-done.7.al1 = f32[4,128,256]{2,1,0:T(8,128)S(1)} collective-permute-done((f32[4,128,256]{2,1,0:T(8,128)S(1)}, f32[4,128,256]{2,1,0:T(8,128)S(1)}, u32[]{:S(2)}, u32[]{:S(2)}) %collective-permute-start.7) | collective-permute-done | bytes 524320 | tf_op jit(solution)/shard_map/ppermute | solution.py:40
  132.7 15.8 %finish.1 = f32[16384,128]{1,0:T(8,128)} custom-call(f32[16384,128]{1,0:T(8,128)S(1)} %bitcast.13, f32[4,128,256]{2,1,0:T(8,128)S(1)} %pad_maximum_fusion.al0, f32[4,128,256]{2,1,0:T(8,128)S(1)} %collective-permute-done.7.al1, f32[4,128,256]{2,1,0:T(8,128)S(1)} %collective-permute-done.8.al2, f32[4,128,256]{2,1,0:T(8,128)S(1)} %collective-permute-done.9.al3, ...), custom_call_target="tpu_custom_call" | custom-call | tf_op jit(solution)/shard_map/finish/pallas_call | solution.py:401
  (48 shorter events, 8.3 us)
Async XLA Ops:
  2.7 10.8 %collective-permute-start.18 = (f32[3,128,128]{2,1,0:T(8,128)}, f32[3,128,128]{2,1,0:T(8,128)S(1)}, u32[]{:S(2)}, u32[]{:S(2)}) collective-permute-start(f32[3,128,128]{2,1,0:T(8,128)} %get-tuple-element.30), channel_id=1, source_target_pairs={{0,64},{1,65},{16,80},{17,81}} | collective-permute-start | bytes 589832 | tf_op jit(solution)/shard_map/ppermute | solution.py:40
  7.9 5.7 %collective-permute-start.17 = (f32[3,128,128]{2,1,0:T(8,128)}, f32[3,128,128]{2,1,0:T(8,128)S(1)}, u32[]{:S(2)}, u32[]{:S(2)}) collective-permute-start(f32[3,128,128]{2,1,0:T(8,128)} %get-tuple-element.30), channel_id=1, source_target_pairs={{0,96},{1,97},{16,112},{17,113}} | collective-permute-start | bytes 589832 | tf_op jit(solution)/shard_map/ppermute | solution.py:40
  9.3 7.3 %collective-permute-start.16 = (f32[3,128,128]{2,1,0:T(8,128)}, f32[3,128,128]{2,1,0:T(8,128)S(1)}, u32[]{:S(2)}, u32[]{:S(2)}) collective-permute-start(f32[3,128,128]{2,1,0:T(8,128)} %get-tuple-element.30), channel_id=1, source_target_pairs={{0,32},{1,33},{16,48},{17,49}} | collective-permute-start | bytes 589832 | tf_op jit(solution)/shard_map/ppermute | solution.py:40
  17.6 8.7 %collective-permute-start.21 = (f32[3,128,128]{2,1,0:T(8,128)S(1)}, f32[3,128,128]{2,1,0:T(8,128)S(1)}, u32[]{:S(2)}, u32[]{:S(2)}) collective-permute-start(f32[3,128,128]{2,1,0:T(8,128)S(1)} %add_select_fusion.2), channel_id=1, source_target_pairs={{0,8},{1,9},{16,24},{17,25},{32,40},{33,41},{48,56},{49,57},{64,72... | collective-permute-start | bytes 589832 | tf_op jit(solution)/shard_map/ppermute | solution.py:40
  18.9 8.7 %collective-permute-start.20 = (f32[3,128,128]{2,1,0:T(8,128)S(1)}, f32[3,128,128]{2,1,0:T(8,128)S(1)}, u32[]{:S(2)}, u32[]{:S(2)}) collective-permute-start(f32[3,128,128]{2,1,0:T(8,128)S(1)} %add_select_fusion.2), channel_id=1, source_target_pairs={{0,12},{1,13},{16,28},{17,29},{32,44},{33,45},{48,60},{49,61},{64,... | collective-permute-start | bytes 589832 | tf_op jit(solution)/shard_map/ppermute | solution.py:40
  20.2 16.3 %collective-permute-start.19 = (f32[3,128,128]{2,1,0:T(8,128)S(1)}, f32[3,128,128]{2,1,0:T(8,128)S(1)}, u32[]{:S(2)}, u32[]{:S(2)}) collective-permute-start(f32[3,128,128]{2,1,0:T(8,128)S(1)} %add_select_fusion.2), channel_id=1, source_target_pairs={{0,4},{1,5},{16,20},{17,21},{32,36},{33,37},{48,52},{49,53},{64,68... | collective-permute-start | bytes 589832 | tf_op jit(solution)/shard_map/ppermute | solution.py:40
  21.5 17.0 %collective-permute-start = (f32[256,256]{1,0:T(8,128)}, f32[256,256]{1,0:T(8,128)S(1)}, u32[]{:S(2)}, u32[]{:S(2)}) collective-permute-start(f32[256,256]{1,0:T(8,128)} %get-tuple-element.23), channel_id=1, source_target_pairs={{0,0},{1,17},{2,34},{3,51},{4,64},{5,81},{6,98},{7,115},{8,8},{9,2... | collective-permute-start | bytes 786440 | tf_op jit(solution)/shard_map/ppermute | solution.py:52
  23.1 16.7 %collective-permute-start.1 = (f32[256,256]{1,0:T(8,128)}, f32[256,256]{1,0:T(8,128)S(1)}, u32[]{:S(2)}, u32[]{:S(2)}) collective-permute-start(f32[256,256]{1,0:T(8,128)} %get-tuple-element.24), channel_id=1, source_target_pairs={{0,1},{1,16},{2,35},{3,50},{4,65},{5,80},{6,99},{7,114},{8,9},{9,2... | collective-permute-start | bytes 786440 | tf_op jit(solution)/shard_map/ppermute | solution.py:52
  26.3 16.3 %collective-permute-start.2 = (f32[256,256]{1,0:T(8,128)}, f32[256,256]{1,0:T(8,128)S(1)}, u32[]{:S(2)}, u32[]{:S(2)}) collective-permute-start(f32[256,256]{1,0:T(8,128)} %get-tuple-element.25), channel_id=1, source_target_pairs={{0,2},{1,19},{2,32},{3,49},{4,66},{5,83},{6,96},{7,113},{8,10},{9,... | collective-permute-start | bytes 786440 | tf_op jit(solution)/shard_map/ppermute | solution.py:52
  27.6 19.0 %collective-permute-start.3 = (f32[256,256]{1,0:T(8,128)}, f32[256,256]{1,0:T(8,128)S(1)}, u32[]{:S(2)}, u32[]{:S(2)}) collective-permute-start(f32[256,256]{1,0:T(8,128)} %get-tuple-element.26), channel_id=1, source_target_pairs={{0,3},{1,18},{2,33},{3,48},{4,67},{5,82},{6,97},{7,112},{8,11},{9,... | collective-permute-start | bytes 786440 | tf_op jit(solution)/shard_map/ppermute | solution.py:52
  36.5 12.9 %collective-permute-start.27 = (f32[3,128,128]{2,1,0:T(8,128)S(1)}, f32[3,128,128]{2,1,0:T(8,128)S(1)}, u32[]{:S(2)}, u32[]{:S(2)}) collective-permute-start(f32[3,128,128]{2,1,0:T(8,128)S(1)} %add_select_fusion.1), channel_id=1, source_target_pairs={{0,3},{1,2},{4,7},{5,6},{8,11},{9,10},{12,15},{13,14},{16,19},{17,... | collective-permute-start | bytes 589832 | tf_op jit(solution)/shard_map/ppermute | solution.py:40
  38.5 12.4 %collective-permute-start.26 = (f32[3,128,128]{2,1,0:T(8,128)S(1)}, f32[3,128,128]{2,1,0:T(8,128)S(1)}, u32[]{:S(2)}, u32[]{:S(2)}) collective-permute-start(f32[3,128,128]{2,1,0:T(8,128)S(1)} %add_select_fusion.1), channel_id=1, source_target_pairs={{0,2},{1,3},{4,6},{5,7},{8,10},{9,11},{12,14},{13,15},{16,18},{17,... | collective-permute-start | bytes 589832 | tf_op jit(solution)/shard_map/ppermute | solution.py:40
  39.8 11.1 %collective-permute-start.25 = (f32[3,128,128]{2,1,0:T(8,128)S(1)}, f32[3,128,128]{2,1,0:T(8,128)S(1)}, u32[]{:S(2)}, u32[]{:S(2)}) collective-permute-start(f32[3,128,128]{2,1,0:T(8,128)S(1)} %add_select_fusion.1), channel_id=1, source_target_pairs={{0,1},{1,0},{4,5},{5,4},{8,9},{9,8},{12,13},{13,12},{16,17},{17,16... | collective-permute-start | bytes 589832 | tf_op jit(solution)/shard_map/ppermute | solution.py:40
  46.7 8.1 %collective-permute-start.12 = (f32[128,256]{1,0:T(8,128)S(1)}, f32[128,256]{1,0:T(8,128)S(1)}, u32[]{:S(2)}, u32[]{:S(2)}) collective-permute-start(f32[128,256]{1,0:T(8,128)S(1)} %get-tuple-element.28), channel_id=1, source_target_pairs={{0,12},{1,13},{2,14},{3,15},{4,8},{5,9},{6,10},{7,11},{8,4},{9,5},... | collective-permute-start | bytes 393224 | tf_op jit(solution)/shard_map/ppermute | solution.py:40
  46.8 8.0 %collective-permute-start.11 = (f32[128,256]{1,0:T(8,128)S(1)}, f32[128,256]{1,0:T(8,128)S(1)}, u32[]{:S(2)}, u32[]{:S(2)}) collective-permute-start(f32[128,256]{1,0:T(8,128)S(1)} %get-tuple-element.28), channel_id=1, source_target_pairs={{0,8},{1,9},{2,10},{3,11},{4,12},{5,13},{6,14},{7,15},{8,0},{9,1},... | collective-permute-start | bytes 393224 | tf_op jit(solution)/shard_map/ppermute | solution.py:40
  49.4 9.4 %collective-permute-start.10 = (f32[128,256]{1,0:T(8,128)S(1)}, f32[128,256]{1,0:T(8,128)S(1)}, u32[]{:S(2)}, u32[]{:S(2)}) collective-permute-start(f32[128,256]{1,0:T(8,128)S(1)} %get-tuple-element.28), channel_id=1, source_target_pairs={{0,4},{1,5},{2,6},{3,7},{4,0},{5,1},{6,2},{7,3},{8,12},{9,13},{10,... | collective-permute-start | bytes 393224 | tf_op jit(solution)/shard_map/ppermute | solution.py:40
  51.0 15.1 %collective-permute-start.28 = (f32[5,128,128]{2,1,0:T(8,128)S(1)}, f32[5,128,128]{2,1,0:T(8,128)S(1)}, u32[]{:S(2)}, u32[]{:S(2)}) collective-permute-start(f32[5,128,128]{2,1,0:T(8,128)S(1)} %pad_maximum_fusion.2.mine_ref), channel_id=1, source_target_pairs={{0,16},{1,17},{2,18},{3,19},{4,20},{5,21},{6,22},{7,23},{8,24},{9,... | collective-permute-start | bytes 983048 | tf_op jit(solution)/shard_map/ppermute | solution.py:40
  51.1 10.1 %collective-permute-start.6 = (f32[128,256]{1,0:T(8,128)S(1)}, f32[128,256]{1,0:T(8,128)S(1)}, u32[]{:S(2)}, u32[]{:S(2)}) collective-permute-start(f32[128,256]{1,0:T(8,128)S(1)} %get-tuple-element.27), channel_id=1, source_target_pairs={{0,3},{1,2},{2,1},{3,0},{4,7},{5,6},{6,5},{7,4},{8,11},{9,10},{10,... | collective-permute-start | bytes 393224 | tf_op jit(solution)/shard_map/ppermute | solution.py:40
  54.7 7.9 %collective-permute-start.5 = (f32[128,256]{1,0:T(8,128)S(1)}, f32[128,256]{1,0:T(8,128)S(1)}, u32[]{:S(2)}, u32[]{:S(2)}) collective-permute-start(f32[128,256]{1,0:T(8,128)S(1)} %get-tuple-element.27), channel_id=1, source_target_pairs={{0,2},{1,3},{2,0},{3,1},{4,6},{5,7},{6,4},{7,5},{8,10},{9,11},{10,... | collective-permute-start | bytes 393224 | tf_op jit(solution)/shard_map/ppermute | solution.py:40
  54.8 8.4 %collective-permute-start.4 = (f32[128,256]{1,0:T(8,128)S(1)}, f32[128,256]{1,0:T(8,128)S(1)}, u32[]{:S(2)}, u32[]{:S(2)}) collective-permute-start(f32[128,256]{1,0:T(8,128)S(1)} %get-tuple-element.27), channel_id=1, source_target_pairs={{0,1},{1,0},{2,3},{3,2},{4,5},{5,4},{6,7},{7,6},{8,9},{9,8},{10,11... | collective-permute-start | bytes 393224 | tf_op jit(solution)/shard_map/ppermute | solution.py:40
  58.8 52.2 %collective-permute-start.15 = (f32[4,128,256]{2,1,0:T(8,128)S(1)}, f32[4,128,256]{2,1,0:T(8,128)S(1)}, u32[]{:S(2)}, u32[]{:S(2)}) collective-permute-start(f32[4,128,256]{2,1,0:T(8,128)S(1)} %pad_maximum_fusion.1.be0), channel_id=1, source_target_pairs={{0,3},{1,2},{2,1},{3,0},{4,7},{5,6},{6,5},{7,4},{8,11},{9,10},{10,... | collective-permute-start | bytes 1572872 | tf_op jit(solution)/shard_map/ppermute | solution.py:40
  61.1 50.1 %collective-permute-start.14 = (f32[4,128,256]{2,1,0:T(8,128)S(1)}, f32[4,128,256]{2,1,0:T(8,128)S(1)}, u32[]{:S(2)}, u32[]{:S(2)}) collective-permute-start(f32[4,128,256]{2,1,0:T(8,128)S(1)} %pad_maximum_fusion.1.be0), channel_id=1, source_target_pairs={{0,2},{1,3},{2,0},{3,1},{4,6},{5,7},{6,4},{7,5},{8,10},{9,11},{10,... | collective-permute-start | bytes 1572872 | tf_op jit(solution)/shard_map/ppermute | solution.py:40
  63.2 47.6 %copy-start = (f32[4,256,256]{2,1,0:T(8,128)S(1)}, f32[4,256,256]{2,1,0:T(8,128)}, u32[]{:S(2)}) copy-start(f32[4,256,256]{2,1,0:T(8,128)} %get-tuple-element.31) | copy-start | bytes 3145732
  63.2 22.5 %collective-permute-start.24 = (f32[4,256,256]{2,1,0:T(8,128)}, f32[4,256,256]{2,1,0:T(8,128)S(1)}, u32[]{:S(2)}, u32[]{:S(2)}) collective-permute-start(f32[4,256,256]{2,1,0:T(8,128)} %get-tuple-element.31), channel_id=1, source_target_pairs={{0,96},{1,97},{2,98},{3,99},{4,100},{5,101},{6,102},{7,103},{8,104... | collective-permute-start | bytes 3145736 | tf_op jit(solution)/shard_map/ppermute | solution.py:40
  64.7 25.1 %collective-permute-start.23 = (f32[4,256,256]{2,1,0:T(8,128)}, f32[4,256,256]{2,1,0:T(8,128)S(1)}, u32[]{:S(2)}, u32[]{:S(2)}) collective-permute-start(f32[4,256,256]{2,1,0:T(8,128)} %get-tuple-element.31), channel_id=1, source_target_pairs={{0,64},{1,65},{2,66},{3,67},{4,68},{5,69},{6,70},{7,71},{8,72},{9,... | collective-permute-start | bytes 3145736 | tf_op jit(solution)/shard_map/ppermute | solution.py:40
  66.1 43.5 %collective-permute-start.22 = (f32[4,256,256]{2,1,0:T(8,128)}, f32[4,256,256]{2,1,0:T(8,128)S(1)}, u32[]{:S(2)}, u32[]{:S(2)}) collective-permute-start(f32[4,256,256]{2,1,0:T(8,128)} %get-tuple-element.31), channel_id=1, source_target_pairs={{0,32},{1,33},{2,34},{3,35},{4,36},{5,37},{6,38},{7,39},{8,40},{9,... | collective-permute-start | bytes 3145736 | tf_op jit(solution)/shard_map/ppermute | solution.py:40
  85.7 35.3 %collective-permute-start.13 = (f32[4,128,256]{2,1,0:T(8,128)S(1)}, f32[4,128,256]{2,1,0:T(8,128)S(1)}, u32[]{:S(2)}, u32[]{:S(2)}) collective-permute-start(f32[4,128,256]{2,1,0:T(8,128)S(1)} %pad_maximum_fusion.1.be0), channel_id=1, source_target_pairs={{0,1},{1,0},{2,3},{3,2},{4,5},{5,4},{6,7},{7,6},{8,9},{9,8},{10,11... | collective-permute-start | bytes 1572872 | tf_op jit(solution)/shard_map/ppermute | solution.py:40
  89.9 31.2 %collective-permute-start.9 = (f32[4,128,256]{2,1,0:T(8,128)S(1)}, f32[4,128,256]{2,1,0:T(8,128)S(1)}, u32[]{:S(2)}, u32[]{:S(2)}) collective-permute-start(f32[4,128,256]{2,1,0:T(8,128)S(1)} %pad_maximum_fusion.al0), channel_id=1, source_target_pairs={{0,12},{1,13},{2,14},{3,15},{4,8},{5,9},{6,10},{7,11},{8,4},{9,5},... | collective-permute-start | bytes 1572872 | tf_op jit(solution)/shard_map/ppermute | solution.py:40
  109.6 16.3 %collective-permute-start.8 = (f32[4,128,256]{2,1,0:T(8,128)S(1)}, f32[4,128,256]{2,1,0:T(8,128)S(1)}, u32[]{:S(2)}, u32[]{:S(2)}) collective-permute-start(f32[4,128,256]{2,1,0:T(8,128)S(1)} %pad_maximum_fusion.al0), channel_id=1, source_target_pairs={{0,8},{1,9},{2,10},{3,11},{4,12},{5,13},{6,14},{7,15},{8,0},{9,1},... | collective-permute-start | bytes 1572872 | tf_op jit(solution)/shard_map/ppermute | solution.py:40
  110.8 21.9 %slice-start = ((s8[8388608]{0:T(1024)(128)(4,1)}), s8[4194304]{0:T(1024)(128)(4,1)S(1)}, s32[]{:S(2)}) async-start(s8[8388608]{0:T(1024)(128)(4,1)} %bitcast.11), calls=%async_computation | async-start | bytes 8388608
  111.1 21.6 %collective-permute-start.7 = (f32[4,128,256]{2,1,0:T(8,128)S(1)}, f32[4,128,256]{2,1,0:T(8,128)S(1)}, u32[]{:S(2)}, u32[]{:S(2)}) collective-permute-start(f32[4,128,256]{2,1,0:T(8,128)S(1)} %pad_maximum_fusion.al0), channel_id=1, source_target_pairs={{0,4},{1,5},{2,6},{3,7},{4,0},{5,1},{6,2},{7,3},{8,12},{9,13},{10,... | collective-permute-start | bytes 1572872 | tf_op jit(solution)/shard_map/ppermute | solution.py:40
  111.3 21.5 %collective-permute-start.29 = (f32[4,256,256]{2,1,0:T(8,128)S(1)}, f32[4,256,256]{2,1,0:T(8,128)S(1)}, u32[]{:S(2)}, u32[]{:S(2)}) collective-permute-start(f32[4,256,256]{2,1,0:T(8,128)S(1)} %add_select_fusion.mine_ref), channel_id=1, source_target_pairs={{0,16},{1,17},{2,18},{3,19},{4,20},{5,21},{6,22},{7,23},{8,24},{9,... | collective-permute-start | bytes 3145736 | tf_op jit(solution)/shard_map/ppermute | solution.py:40
  (1 other events, 21.3 us)

commit v3 on v2

--- a/solution.py
+++ b/solution.py
@@ -237,13 +237,13 @@
 
     pl.when(k == 0)(lambda: load(mine_ref, other_ref))
     pl.when(k == 1)(lambda: load(other_ref, mine_ref))
-    factor_steps(0, 2, s_ref, inv_ref, *work)
+    factor_steps(0, 3, s_ref, inv_ref, *work)
 
 
 def chol_last_kernel(s_in, inv_in, s_ref, inv_ref, *work):
     s_ref[...] = s_in[...]
     inv_ref[...] = inv_in[...]
-    factor_steps(2, 4, s_ref, inv_ref, *work)
+    factor_steps(3, 4, s_ref, inv_ref, *work)
 
 
 TILES = (4, 4, HALF, HALF)
@@ -326,11 +326,15 @@
     pl.when(k == 0)(lambda: columns(mine_ref, other_ref))
     pl.when(k == 1)(lambda: columns(other_ref, mine_ref))
 
-    def panel(even, odd, places):
-        first = z % 2
-        total = three_nt(split(even), (lh_ref[first, 0], lh_ref[first, 1])) + three_nt(
-            split(odd), (lh_ref[1 - first, 0], lh_ref[1 - first, 1])
-        )
+    def panel(left, right, places):
+        def tile(h, i):
+            at = slice(i * NB, (i + 1) * NB)
+            return lh_ref[h, 0, at], lh_ref[h, 1, at]
+
+        left, right = split(left), split(right)
+        up = three_nt(left, tile(0, 0))
+        down = three_nt(left, tile(0, 1)) + three_nt(right, tile(1, 1))
+        total = jnp.concatenate([up, down], axis=1)
         for i, (t, half) in enumerate(places):
             at = slice(half * HALF, (half + 1) * HALF)
             part = total[i * HALF:(i + 1) * HALF]
@@ -340,19 +344,24 @@
             pk_ref[t, at, W:2 * W] = hi
             pk_ref[t, at, 2 * W:3 * W] = lo
 
-    for pair in range(2):
-        panel(
-            alphas[2 * pair][...].reshape(W, NB),
-            alphas[2 * pair + 1][...].reshape(W, NB),
-            [(pair * 4 + ex, 0) for ex in range(4)],
-        )
-    for half in range(2):
-        pick = [(ex, pair) for ex in (2 * half, 2 * half + 1) for pair in range(2)]
-        panel(
-            jnp.concatenate([betas[ex][2 * pair] for ex, pair in pick], axis=0),
-            jnp.concatenate([betas[ex][2 * pair + 1] for ex, pair in pick], axis=0),
-            [(pair * 4 + ex, 1) for ex, pair in pick],
-        )
+    def panels(first):
+        for pair in range(2):
+            ez = 2 * pair + first
+            panel(
+                alphas[ez][...].reshape(W, NB),
+                alphas[ez ^ 1][...].reshape(W, NB),
+                [(pair * 4 + ex, 0) for ex in range(4)],
+            )
+        for half in range(2):
+            pick = [(ex, pair) for ex in (2 * half, 2 * half + 1) for pair in range(2)]
+            panel(
+                jnp.concatenate([betas[ex][2 * pair + first] for ex, pair in pick], axis=0),
+                jnp.concatenate([betas[ex][2 * pair + (1 - first)] for ex, pair in pick], axis=0),
+                [(pair * 4 + ex, 1) for ex, pair in pick],
+            )
+
+    pl.when(z % 2 == 0)(lambda: panels(0))
+    pl.when(z % 2 == 1)(lambda: panels(1))
 
     def step(u, carry):
         left = pk_ref[pl.ds(2 * u, 2)].reshape(2 * NB, 3 * W)
@@ -455,12 +464,12 @@
     got = [swap(late, y=e, only=lambda yy, kk, zz, xx: yy == 0) for e in (1, 2, 3)]
 
     own = after(own, along_x, along_z)
-    lower, inverse = chol(chol_first_kernel, (own, other), 12 * FLOPS_US)
+    lower, inverse = chol(chol_first_kernel, (own, other), 15 * FLOPS_US)
     got = lax.optimization_barrier((*got, lower))[:3]
     mine = jnp.where(y == 0, blocks, got[0] + got[1] + got[2])
     mine_other = swap(mine, k=1)
     lower = after(lower, mine)
-    lower, inverse = chol(chol_last_kernel, (lower, inverse), 12 * FLOPS_US)
+    lower, inverse = chol(chol_last_kernel, (lower, inverse), 5 * FLOPS_US)
     out = finish(view, alphas, betas, mine, mine_other, lower, inverse)
     return out.reshape(matrix.shape)
 

time: 151 us -> 156 us (1.033)
  waiting for transfers between devices: 58.5 us -> 62.8 us
  starting transfers between devices: 50.4 us -> 53.1 us
    ppermute x26, waiting for transfers between devices: 54.6 us -> 58.8 us  [swap(): return lax.ppermute(value, AXES, pairs)]
    ppermute x26, starting transfers between devices: 35.5 us -> 38.2 us  [swap(): return lax.ppermute(value, AXES, pairs)]
  transfers between devices with their start and end apart: 30 -> 30, of which waited for: 13 -> 14; matrix products, arithmetic and copies ran while one was open for 0% -> 0% of each run, Pallas kernels for 13% -> 12%
where the time goes in v3:
time: 156 us; the launch traced here: 155 us
  waiting for transfers between devices  62.8 us (40%)
  starting transfers between devices  53.1 us (34%)
  Pallas kernels  36.8 us (24%)
    ppermute x26, waiting for transfers between devices, swap(): return lax.ppermute(value, AXES, pairs)  58.8 us
    ppermute x26, starting transfers between devices, swap(): return lax.ppermute(value, AXES, pairs)  38.2 us
    pallas_call x2, Pallas kernels, chol(): pl.pallas_call(kernel, in_specs=[VMEM, VMEM], out_specs=[VMEM, VMEM], out...  18.9 us
    pallas_call x1, Pallas kernels, finish(): pl.pallas_call(finish_kernel, in_specs=[VMEM] * 13, out_specs=hbm, out_sh...  15.1 us
    ppermute x4, starting transfers between devices, scatter(): return lax.ppermute(value, AXES, pairs)  14.9 us
    ppermute x4, waiting for transfers between devices, scatter(): return lax.ppermute(value, AXES, pairs)  3.97 us
  transfers between devices with their start and end apart: 30, of which 14 were waited for; matrix products, arithmetic and copies ran while one was open for 0% of the time, Pallas kernels for 12%

profile of v3, /device:TPU:0, one launch (start us, length us, event | category | flops | bytes accessed | tf_op | source)
XLA Modules:
  0.0 154.7 jit_solution(6349553325470786521)
XLA Ops:
  0.0 2.7 %extract.1 = (f32[3,128,128]{2,1,0:T(8,128)}, f32[4,256,256]{2,1,0:T(8,128)}, f32[256,256]{1,0:T(8,128)}, f32[256,256]{1,0:T(8,128)}, f32[256,256]{1,0:T(8,128)}, /*index=5*/f32[256,256]{1,0:T(8,128)}) custom-call(f32[16384,128]{1,0:T(8,128)} %bitcast.10), custom_call_target="tpu_custom_call" | custom-call | tf_op jit(solution)/shard_map/extract/pallas_call | solution.py:93
  2.7 5.2 %collective-permute-start.18 = (f32[3,128,128]{2,1,0:T(8,128)}, f32[3,128,128]{2,1,0:T(8,128)S(1)}, u32[]{:S(2)}, u32[]{:S(2)}) collective-permute-start(f32[3,128,128]{2,1,0:T(8,128)} %get-tuple-element.30), channel_id=1, source_target_pairs={{0,64},{1,65},{16,80},{17,81}} | collective-permute-start | bytes 589832 | tf_op jit(solution)/shard_map/ppermute | solution.py:40
  10.6 2.9 %collective-permute-done.18 = f32[3,128,128]{2,1,0:T(8,128)S(1)} collective-permute-done((f32[3,128,128]{2,1,0:T(8,128)}, f32[3,128,128]{2,1,0:T(8,128)S(1)}, u32[]{:S(2)}, u32[]{:S(2)}) %collective-permute-start.18) | collective-permute-done | bytes 196640 | tf_op jit(solution)/shard_map/ppermute | solution.py:40
  13.7 2.9 %collective-permute-done.16 = f32[3,128,128]{2,1,0:T(8,128)S(1)} collective-permute-done((f32[3,128,128]{2,1,0:T(8,128)}, f32[3,128,128]{2,1,0:T(8,128)S(1)}, u32[]{:S(2)}, u32[]{:S(2)}) %collective-permute-start.16) | collective-permute-done | bytes 196640 | tf_op jit(solution)/shard_map/ppermute | solution.py:40
  17.6 1.3 collective-permute-start.21
  21.5 1.6 %collective-permute-start = (f32[256,256]{1,0:T(8,128)}, f32[256,256]{1,0:T(8,128)S(1)}, u32[]{:S(2)}, u32[]{:S(2)}) collective-permute-start(f32[256,256]{1,0:T(8,128)} %get-tuple-element.23), channel_id=1, source_target_pairs={{0,0},{1,17},{2,34},{3,51},{4,64},{5,81},{6,98},{7,115},{8,8},{9,2... | collective-permute-start | bytes 786440 | tf_op jit(solution)/shard_map/ppermute | solution.py:52
  23.1 3.1 %collective-permute-start.1 = (f32[256,256]{1,0:T(8,128)}, f32[256,256]{1,0:T(8,128)S(1)}, u32[]{:S(2)}, u32[]{:S(2)}) collective-permute-start(f32[256,256]{1,0:T(8,128)} %get-tuple-element.24), channel_id=1, source_target_pairs={{0,1},{1,16},{2,35},{3,50},{4,65},{5,80},{6,99},{7,114},{8,9},{9,2... | collective-permute-start | bytes 786440 | tf_op jit(solution)/shard_map/ppermute | solution.py:52
  26.3 1.3 collective-permute-start.2
  27.6 8.9 %collective-permute-start.3 = (f32[256,256]{1,0:T(8,128)}, f32[256,256]{1,0:T(8,128)S(1)}, u32[]{:S(2)}, u32[]{:S(2)}) collective-permute-start(f32[256,256]{1,0:T(8,128)} %get-tuple-element.26), channel_id=1, source_target_pairs={{0,3},{1,18},{2,33},{3,48},{4,67},{5,82},{6,97},{7,112},{8,11},{9,... | collective-permute-start | bytes 786440 | tf_op jit(solution)/shard_map/ppermute | solution.py:52
  36.5 1.9 %collective-permute-start.27 = (f32[3,128,128]{2,1,0:T(8,128)S(1)}, f32[3,128,128]{2,1,0:T(8,128)S(1)}, u32[]{:S(2)}, u32[]{:S(2)}) collective-permute-start(f32[3,128,128]{2,1,0:T(8,128)S(1)} %add_select_fusion.1), channel_id=1, source_target_pairs={{0,3},{1,2},{4,7},{5,6},{8,11},{9,10},{12,15},{13,14},{16,19},{17,... | collective-permute-start | bytes 589832 | tf_op jit(solution)/shard_map/ppermute | solution.py:40
  39.8 2.8 %collective-permute-start.25 = (f32[3,128,128]{2,1,0:T(8,128)S(1)}, f32[3,128,128]{2,1,0:T(8,128)S(1)}, u32[]{:S(2)}, u32[]{:S(2)}) collective-permute-start(f32[3,128,128]{2,1,0:T(8,128)S(1)} %add_select_fusion.1), channel_id=1, source_target_pairs={{0,1},{1,0},{4,5},{5,4},{8,9},{9,8},{12,13},{13,12},{16,17},{17,16... | collective-permute-start | bytes 589832 | tf_op jit(solution)/shard_map/ppermute | solution.py:40
  42.6 4.0 %collective-permute-done.3.s3 = f32[256,256]{1,0:T(8,128)S(1)} collective-permute-done((f32[256,256]{1,0:T(8,128)}, f32[256,256]{1,0:T(8,128)S(1)}, u32[]{:S(2)}, u32[]{:S(2)}) %collective-permute-start.3) | collective-permute-done | bytes 262176 | tf_op jit(solution)/shard_map/ppermute | solution.py:52
  46.9 2.5 %collective-permute-done.27 = f32[3,128,128]{2,1,0:T(8,128)S(1)} collective-permute-done((f32[3,128,128]{2,1,0:T(8,128)S(1)}, f32[3,128,128]{2,1,0:T(8,128)S(1)}, u32[]{:S(2)}, u32[]{:S(2)}) %collective-permute-start.27) | collective-permute-done | bytes 196640 | tf_op jit(solution)/shard_map/ppermute | solution.py:40
  49.4 1.4 collective-permute-start.10
  51.1 3.7 %collective-permute-start.6 = (f32[128,256]{1,0:T(8,128)S(1)}, f32[128,256]{1,0:T(8,128)S(1)}, u32[]{:S(2)}, u32[]{:S(2)}) collective-permute-start(f32[128,256]{1,0:T(8,128)S(1)} %get-tuple-element.27), channel_id=1, source_target_pairs={{0,3},{1,2},{2,1},{3,0},{4,7},{5,6},{6,5},{7,4},{8,11},{9,10},{10,... | collective-permute-start | bytes 393224 | tf_op jit(solution)/shard_map/ppermute | solution.py:40
  54.8 4.0 %collective-permute-start.4 = (f32[128,256]{1,0:T(8,128)S(1)}, f32[128,256]{1,0:T(8,128)S(1)}, u32[]{:S(2)}, u32[]{:S(2)}) collective-permute-start(f32[128,256]{1,0:T(8,128)S(1)} %get-tuple-element.27), channel_id=1, source_target_pairs={{0,1},{1,0},{2,3},{3,2},{4,5},{5,4},{6,7},{7,6},{8,9},{9,8},{10,11... | collective-permute-start | bytes 393224 | tf_op jit(solution)/shard_map/ppermute | solution.py:40
  59.0 2.2 %collective-permute-done.6 = f32[128,256]{1,0:T(8,128)S(1)} collective-permute-done((f32[128,256]{1,0:T(8,128)S(1)}, f32[128,256]{1,0:T(8,128)S(1)}, u32[]{:S(2)}, u32[]{:S(2)}) %collective-permute-start.6) | collective-permute-done | bytes 131104 | tf_op jit(solution)/shard_map/ppermute | solution.py:40
  61.1 1.5 collective-permute-done.5
  63.2 1.5 collective-permute-start.24
  64.7 1.4 collective-permute-start.23
  66.1 1.4 collective-permute-start.22
  67.5 14.3 %shard_map.17 = (f32[4,4,128,128]{3,2,1,0:T(8,128)S(1)}, f32[4,4,128,128]{3,2,1,0:T(8,128)S(1)}) custom-call(f32[5,128,128]{2,1,0:T(8,128)S(1)} %pad_maximum_fusion.2.mine_ref, f32[5,128,128]{2,1,0:T(8,128)S(1)} %collective-permute-done.28.other_ref), custom_call_target="tpu_custom_call" | custom-call | flops 15000000512 | tf_op jit(solution)/shard_map/pallas_call | solution.py:254
  81.8 3.9 %collective-permute-done.24 = f32[4,256,256]{2,1,0:T(8,128)S(1)} collective-permute-done((f32[4,256,256]{2,1,0:T(8,128)}, f32[4,256,256]{2,1,0:T(8,128)S(1)}, u32[]{:S(2)}, u32[]{:S(2)}) %collective-permute-start.24) | collective-permute-done | bytes 1048608 | tf_op jit(solution)/shard_map/ppermute | solution.py:40
  85.7 4.1 %collective-permute-done.23 = f32[4,256,256]{2,1,0:T(8,128)S(1)} collective-permute-done((f32[4,256,256]{2,1,0:T(8,128)}, f32[4,256,256]{2,1,0:T(8,128)S(1)}, u32[]{:S(2)}, u32[]{:S(2)}) %collective-permute-start.23) | collective-permute-done | bytes 1048608 | tf_op jit(solution)/shard_map/ppermute | solution.py:40
  89.9 19.7 %collective-permute-done.22 = f32[4,256,256]{2,1,0:T(8,128)S(1)} collective-permute-done((f32[4,256,256]{2,1,0:T(8,128)}, f32[4,256,256]{2,1,0:T(8,128)S(1)}, u32[]{:S(2)}, u32[]{:S(2)}) %collective-permute-start.22) | collective-permute-done | bytes 1048608 | tf_op jit(solution)/shard_map/ppermute | solution.py:40
  109.9 2.5 %collective-permute-start.13 = (f32[4,128,256]{2,1,0:T(8,128)S(1)}, f32[4,128,256]{2,1,0:T(8,128)S(1)}, u32[]{:S(2)}, u32[]{:S(2)}) collective-permute-start(f32[4,128,256]{2,1,0:T(8,128)S(1)} %pad_maximum_fusion.1.be0), channel_id=1, source_target_pairs={{0,1},{1,0},{2,3},{3,2},{4,5},{5,4},{6,7},{7,6},{8,9},{9,8},{10,11... | collective-permute-start | bytes 1572872 | tf_op jit(solution)/shard_map/ppermute | solution.py:40
  112.4 1.5 collective-permute-start.9
  113.9 2.7 %collective-permute-start.8 = (f32[4,128,256]{2,1,0:T(8,128)S(1)}, f32[4,128,256]{2,1,0:T(8,128)S(1)}, u32[]{:S(2)}, u32[]{:S(2)}) collective-permute-start(f32[4,128,256]{2,1,0:T(8,128)S(1)} %pad_maximum_fusion.al0), channel_id=1, source_target_pairs={{0,8},{1,9},{2,10},{3,11},{4,12},{5,13},{6,14},{7,15},{8,0},{9,1},... | collective-permute-start | bytes 1572872 | tf_op jit(solution)/shard_map/ppermute | solution.py:40
  116.6 4.5 %shard_map.18 = (f32[4,4,128,128]{3,2,1,0:T(8,128)S(1)}, f32[4,4,128,128]{3,2,1,0:T(8,128)S(1)}) custom-call(f32[4,4,128,128]{3,2,1,0:T(8,128)S(1)} %get-tuple-element.37.s_in, f32[4,4,128,128]{3,2,1,0:T(8,128)S(1)} %get-tuple-element.38.inv_in), custom_call_target="tpu_custom_call" | custom-call | flops 5000000000 | tf_op jit(solution)/shard_map/pallas_call | solution.py:254
  121.1 3.8 %collective-permute-done.13.be1 = f32[4,128,256]{2,1,0:T(8,128)S(1)} collective-permute-done((f32[4,128,256]{2,1,0:T(8,128)S(1)}, f32[4,128,256]{2,1,0:T(8,128)S(1)}, u32[]{:S(2)}, u32[]{:S(2)}) %collective-permute-start.13) | collective-permute-done | bytes 524320 | tf_op jit(solution)/shard_map/ppermute | solution.py:40
  124.9 13.9 %collective-permute-done.9.al3 = f32[4,128,256]{2,1,0:T(8,128)S(1)} collective-permute-done((f32[4,128,256]{2,1,0:T(8,128)S(1)}, f32[4,128,256]{2,1,0:T(8,128)S(1)}, u32[]{:S(2)}, u32[]{:S(2)}) %collective-permute-start.9) | collective-permute-done | bytes 524320 | tf_op jit(solution)/shard_map/ppermute | solution.py:40
  139.5 15.1 %finish.1 = f32[16384,128]{1,0:T(8,128)} custom-call(f32[16384,128]{1,0:T(8,128)S(1)} %bitcast.13, f32[4,128,256]{2,1,0:T(8,128)S(1)} %pad_maximum_fusion.al0, f32[4,128,256]{2,1,0:T(8,128)S(1)} %collective-permute-done.7.al1, f32[4,128,256]{2,1,0:T(8,128)S(1)} %collective-permute-done.8.al2, f32[4,128,256]{2,1,0:T(8,128)S(1)} %collective-permute-done.9.al3, ...), custom_call_target="tpu_custom_call" | custom-call | tf_op jit(solution)/shard_map/finish/pallas_call | solution.py:410
  (48 shorter events, 10.0 us)
Async XLA Ops:
  2.7 10.8 %collective-permute-start.18 = (f32[3,128,128]{2,1,0:T(8,128)}, f32[3,128,128]{2,1,0:T(8,128)S(1)}, u32[]{:S(2)}, u32[]{:S(2)}) collective-permute-start(f32[3,128,128]{2,1,0:T(8,128)} %get-tuple-element.30), channel_id=1, source_target_pairs={{0,64},{1,65},{16,80},{17,81}} | collective-permute-start | bytes 589832 | tf_op jit(solution)/shard_map/ppermute | solution.py:40
  7.9 5.7 %collective-permute-start.17 = (f32[3,128,128]{2,1,0:T(8,128)}, f32[3,128,128]{2,1,0:T(8,128)S(1)}, u32[]{:S(2)}, u32[]{:S(2)}) collective-permute-start(f32[3,128,128]{2,1,0:T(8,128)} %get-tuple-element.30), channel_id=1, source_target_pairs={{0,96},{1,97},{16,112},{17,113}} | collective-permute-start | bytes 589832 | tf_op jit(solution)/shard_map/ppermute | solution.py:40
  9.3 7.3 %collective-permute-start.16 = (f32[3,128,128]{2,1,0:T(8,128)}, f32[3,128,128]{2,1,0:T(8,128)S(1)}, u32[]{:S(2)}, u32[]{:S(2)}) collective-permute-start(f32[3,128,128]{2,1,0:T(8,128)} %get-tuple-element.30), channel_id=1, source_target_pairs={{0,32},{1,33},{16,48},{17,49}} | collective-permute-start | bytes 589832 | tf_op jit(solution)/shard_map/ppermute | solution.py:40
  17.6 8.7 %collective-permute-start.21 = (f32[3,128,128]{2,1,0:T(8,128)S(1)}, f32[3,128,128]{2,1,0:T(8,128)S(1)}, u32[]{:S(2)}, u32[]{:S(2)}) collective-permute-start(f32[3,128,128]{2,1,0:T(8,128)S(1)} %add_select_fusion.2), channel_id=1, source_target_pairs={{0,8},{1,9},{16,24},{17,25},{32,40},{33,41},{48,56},{49,57},{64,72... | collective-permute-start | bytes 589832 | tf_op jit(solution)/shard_map/ppermute | solution.py:40
  18.9 8.7 %collective-permute-start.20 = (f32[3,128,128]{2,1,0:T(8,128)S(1)}, f32[3,128,128]{2,1,0:T(8,128)S(1)}, u32[]{:S(2)}, u32[]{:S(2)}) collective-permute-start(f32[3,128,128]{2,1,0:T(8,128)S(1)} %add_select_fusion.2), channel_id=1, source_target_pairs={{0,12},{1,13},{16,28},{17,29},{32,44},{33,45},{48,60},{49,61},{64,... | collective-permute-start | bytes 589832 | tf_op jit(solution)/shard_map/ppermute | solution.py:40
  20.2 16.3 %collective-permute-start.19 = (f32[3,128,128]{2,1,0:T(8,128)S(1)}, f32[3,128,128]{2,1,0:T(8,128)S(1)}, u32[]{:S(2)}, u32[]{:S(2)}) collective-permute-start(f32[3,128,128]{2,1,0:T(8,128)S(1)} %add_select_fusion.2), channel_id=1, source_target_pairs={{0,4},{1,5},{16,20},{17,21},{32,36},{33,37},{48,52},{49,53},{64,68... | collective-permute-start | bytes 589832 | tf_op jit(solution)/shard_map/ppermute | solution.py:40
  21.5 17.0 %collective-permute-start = (f32[256,256]{1,0:T(8,128)}, f32[256,256]{1,0:T(8,128)S(1)}, u32[]{:S(2)}, u32[]{:S(2)}) collective-permute-start(f32[256,256]{1,0:T(8,128)} %get-tuple-element.23), channel_id=1, source_target_pairs={{0,0},{1,17},{2,34},{3,51},{4,64},{5,81},{6,98},{7,115},{8,8},{9,2... | collective-permute-start | bytes 786440 | tf_op jit(solution)/shard_map/ppermute | solution.py:52
  23.1 16.7 %collective-permute-start.1 = (f32[256,256]{1,0:T(8,128)}, f32[256,256]{1,0:T(8,128)S(1)}, u32[]{:S(2)}, u32[]{:S(2)}) collective-permute-start(f32[256,256]{1,0:T(8,128)} %get-tuple-element.24), channel_id=1, source_target_pairs={{0,1},{1,16},{2,35},{3,50},{4,65},{5,80},{6,99},{7,114},{8,9},{9,2... | collective-permute-start | bytes 786440 | tf_op jit(solution)/shard_map/ppermute | solution.py:52
  26.3 16.3 %collective-permute-start.2 = (f32[256,256]{1,0:T(8,128)}, f32[256,256]{1,0:T(8,128)S(1)}, u32[]{:S(2)}, u32[]{:S(2)}) collective-permute-start(f32[256,256]{1,0:T(8,128)} %get-tuple-element.25), channel_id=1, source_target_pairs={{0,2},{1,19},{2,32},{3,49},{4,66},{5,83},{6,96},{7,113},{8,10},{9,... | collective-permute-start | bytes 786440 | tf_op jit(solution)/shard_map/ppermute | solution.py:52
  27.6 19.0 %collective-permute-start.3 = (f32[256,256]{1,0:T(8,128)}, f32[256,256]{1,0:T(8,128)S(1)}, u32[]{:S(2)}, u32[]{:S(2)}) collective-permute-start(f32[256,256]{1,0:T(8,128)} %get-tuple-element.26), channel_id=1, source_target_pairs={{0,3},{1,18},{2,33},{3,48},{4,67},{5,82},{6,97},{7,112},{8,11},{9,... | collective-permute-start | bytes 786440 | tf_op jit(solution)/shard_map/ppermute | solution.py:52
  36.5 12.9 %collective-permute-start.27 = (f32[3,128,128]{2,1,0:T(8,128)S(1)}, f32[3,128,128]{2,1,0:T(8,128)S(1)}, u32[]{:S(2)}, u32[]{:S(2)}) collective-permute-start(f32[3,128,128]{2,1,0:T(8,128)S(1)} %add_select_fusion.1), channel_id=1, source_target_pairs={{0,3},{1,2},{4,7},{5,6},{8,11},{9,10},{12,15},{13,14},{16,19},{17,... | collective-permute-start | bytes 589832 | tf_op jit(solution)/shard_map/ppermute | solution.py:40
  38.5 12.4 %collective-permute-start.26 = (f32[3,128,128]{2,1,0:T(8,128)S(1)}, f32[3,128,128]{2,1,0:T(8,128)S(1)}, u32[]{:S(2)}, u32[]{:S(2)}) collective-permute-start(f32[3,128,128]{2,1,0:T(8,128)S(1)} %add_select_fusion.1), channel_id=1, source_target_pairs={{0,2},{1,3},{4,6},{5,7},{8,10},{9,11},{12,14},{13,15},{16,18},{17,... | collective-permute-start | bytes 589832 | tf_op jit(solution)/shard_map/ppermute | solution.py:40
  39.8 11.1 %collective-permute-start.25 = (f32[3,128,128]{2,1,0:T(8,128)S(1)}, f32[3,128,128]{2,1,0:T(8,128)S(1)}, u32[]{:S(2)}, u32[]{:S(2)}) collective-permute-start(f32[3,128,128]{2,1,0:T(8,128)S(1)} %add_select_fusion.1), channel_id=1, source_target_pairs={{0,1},{1,0},{4,5},{5,4},{8,9},{9,8},{12,13},{13,12},{16,17},{17,16... | collective-permute-start | bytes 589832 | tf_op jit(solution)/shard_map/ppermute | solution.py:40
  46.7 8.1 %collective-permute-start.12 = (f32[128,256]{1,0:T(8,128)S(1)}, f32[128,256]{1,0:T(8,128)S(1)}, u32[]{:S(2)}, u32[]{:S(2)}) collective-permute-start(f32[128,256]{1,0:T(8,128)S(1)} %get-tuple-element.28), channel_id=1, source_target_pairs={{0,12},{1,13},{2,14},{3,15},{4,8},{5,9},{6,10},{7,11},{8,4},{9,5},... | collective-permute-start | bytes 393224 | tf_op jit(solution)/shard_map/ppermute | solution.py:40
  46.8 8.0 %collective-permute-start.11 = (f32[128,256]{1,0:T(8,128)S(1)}, f32[128,256]{1,0:T(8,128)S(1)}, u32[]{:S(2)}, u32[]{:S(2)}) collective-permute-start(f32[128,256]{1,0:T(8,128)S(1)} %get-tuple-element.28), channel_id=1, source_target_pairs={{0,8},{1,9},{2,10},{3,11},{4,12},{5,13},{6,14},{7,15},{8,0},{9,1},... | collective-permute-start | bytes 393224 | tf_op jit(solution)/shard_map/ppermute | solution.py:40
  49.4 9.4 %collective-permute-start.10 = (f32[128,256]{1,0:T(8,128)S(1)}, f32[128,256]{1,0:T(8,128)S(1)}, u32[]{:S(2)}, u32[]{:S(2)}) collective-permute-start(f32[128,256]{1,0:T(8,128)S(1)} %get-tuple-element.28), channel_id=1, source_target_pairs={{0,4},{1,5},{2,6},{3,7},{4,0},{5,1},{6,2},{7,3},{8,12},{9,13},{10,... | collective-permute-start | bytes 393224 | tf_op jit(solution)/shard_map/ppermute | solution.py:40
  51.0 15.1 %collective-permute-start.28 = (f32[5,128,128]{2,1,0:T(8,128)S(1)}, f32[5,128,128]{2,1,0:T(8,128)S(1)}, u32[]{:S(2)}, u32[]{:S(2)}) collective-permute-start(f32[5,128,128]{2,1,0:T(8,128)S(1)} %pad_maximum_fusion.2.mine_ref), channel_id=1, source_target_pairs={{0,16},{1,17},{2,18},{3,19},{4,20},{5,21},{6,22},{7,23},{8,24},{9,... | collective-permute-start | bytes 983048 | tf_op jit(solution)/shard_map/ppermute | solution.py:40
  51.1 10.1 %collective-permute-start.6 = (f32[128,256]{1,0:T(8,128)S(1)}, f32[128,256]{1,0:T(8,128)S(1)}, u32[]{:S(2)}, u32[]{:S(2)}) collective-permute-start(f32[128,256]{1,0:T(8,128)S(1)} %get-tuple-element.27), channel_id=1, source_target_pairs={{0,3},{1,2},{2,1},{3,0},{4,7},{5,6},{6,5},{7,4},{8,11},{9,10},{10,... | collective-permute-start | bytes 393224 | tf_op jit(solution)/shard_map/ppermute | solution.py:40
  54.7 7.9 %collective-permute-start.5 = (f32[128,256]{1,0:T(8,128)S(1)}, f32[128,256]{1,0:T(8,128)S(1)}, u32[]{:S(2)}, u32[]{:S(2)}) collective-permute-start(f32[128,256]{1,0:T(8,128)S(1)} %get-tuple-element.27), channel_id=1, source_target_pairs={{0,2},{1,3},{2,0},{3,1},{4,6},{5,7},{6,4},{7,5},{8,10},{9,11},{10,... | collective-permute-start | bytes 393224 | tf_op jit(solution)/shard_map/ppermute | solution.py:40
  54.8 8.4 %collective-permute-start.4 = (f32[128,256]{1,0:T(8,128)S(1)}, f32[128,256]{1,0:T(8,128)S(1)}, u32[]{:S(2)}, u32[]{:S(2)}) collective-permute-start(f32[128,256]{1,0:T(8,128)S(1)} %get-tuple-element.27), channel_id=1, source_target_pairs={{0,1},{1,0},{2,3},{3,2},{4,5},{5,4},{6,7},{7,6},{8,9},{9,8},{10,11... | collective-permute-start | bytes 393224 | tf_op jit(solution)/shard_map/ppermute | solution.py:40
  58.8 55.1 %collective-permute-start.15 = (f32[4,128,256]{2,1,0:T(8,128)S(1)}, f32[4,128,256]{2,1,0:T(8,128)S(1)}, u32[]{:S(2)}, u32[]{:S(2)}) collective-permute-start(f32[4,128,256]{2,1,0:T(8,128)S(1)} %pad_maximum_fusion.1.be0), channel_id=1, source_target_pairs={{0,3},{1,2},{2,1},{3,0},{4,7},{5,6},{6,5},{7,4},{8,11},{9,10},{10,... | collective-permute-start | bytes 1572872 | tf_op jit(solution)/shard_map/ppermute | solution.py:40
  61.1 55.5 %collective-permute-start.14 = (f32[4,128,256]{2,1,0:T(8,128)S(1)}, f32[4,128,256]{2,1,0:T(8,128)S(1)}, u32[]{:S(2)}, u32[]{:S(2)}) collective-permute-start(f32[4,128,256]{2,1,0:T(8,128)S(1)} %pad_maximum_fusion.1.be0), channel_id=1, source_target_pairs={{0,2},{1,3},{2,0},{3,1},{4,6},{5,7},{6,4},{7,5},{8,10},{9,11},{10,... | collective-permute-start | bytes 1572872 | tf_op jit(solution)/shard_map/ppermute | solution.py:40
  63.2 46.3 %copy-start = (f32[4,256,256]{2,1,0:T(8,128)S(1)}, f32[4,256,256]{2,1,0:T(8,128)}, u32[]{:S(2)}) copy-start(f32[4,256,256]{2,1,0:T(8,128)} %get-tuple-element.31) | copy-start | bytes 3145732
  63.2 22.5 %collective-permute-start.24 = (f32[4,256,256]{2,1,0:T(8,128)}, f32[4,256,256]{2,1,0:T(8,128)S(1)}, u32[]{:S(2)}, u32[]{:S(2)}) collective-permute-start(f32[4,256,256]{2,1,0:T(8,128)} %get-tuple-element.31), channel_id=1, source_target_pairs={{0,96},{1,97},{2,98},{3,99},{4,100},{5,101},{6,102},{7,103},{8,104... | collective-permute-start | bytes 3145736 | tf_op jit(solution)/shard_map/ppermute | solution.py:40
  64.7 25.1 %collective-permute-start.23 = (f32[4,256,256]{2,1,0:T(8,128)}, f32[4,256,256]{2,1,0:T(8,128)S(1)}, u32[]{:S(2)}, u32[]{:S(2)}) collective-permute-start(f32[4,256,256]{2,1,0:T(8,128)} %get-tuple-element.31), channel_id=1, source_target_pairs={{0,64},{1,65},{2,66},{3,67},{4,68},{5,69},{6,70},{7,71},{8,72},{9,... | collective-permute-start | bytes 3145736 | tf_op jit(solution)/shard_map/ppermute | solution.py:40
  66.1 43.5 %collective-permute-start.22 = (f32[4,256,256]{2,1,0:T(8,128)}, f32[4,256,256]{2,1,0:T(8,128)S(1)}, u32[]{:S(2)}, u32[]{:S(2)}) collective-permute-start(f32[4,256,256]{2,1,0:T(8,128)} %get-tuple-element.31), channel_id=1, source_target_pairs={{0,32},{1,33},{2,34},{3,35},{4,36},{5,37},{6,38},{7,39},{8,40},{9,... | collective-permute-start | bytes 3145736 | tf_op jit(solution)/shard_map/ppermute | solution.py:40
  109.6 29.9 %slice-start = ((s8[8388608]{0:T(1024)(128)(4,1)}), s8[4194304]{0:T(1024)(128)(4,1)S(1)}, s32[]{:S(2)}) async-start(s8[8388608]{0:T(1024)(128)(4,1)} %bitcast.11), calls=%async_computation | async-start | bytes 8388608
  109.8 29.6 %collective-permute-start.29 = (f32[4,256,256]{2,1,0:T(8,128)S(1)}, f32[4,256,256]{2,1,0:T(8,128)S(1)}, u32[]{:S(2)}, u32[]{:S(2)}) collective-permute-start(f32[4,256,256]{2,1,0:T(8,128)S(1)} %add_select_fusion.mine_ref), channel_id=1, source_target_pairs={{0,16},{1,17},{2,18},{3,19},{4,20},{5,21},{6,22},{7,23},{8,24},{9,... | collective-permute-start | bytes 3145736 | tf_op jit(solution)/shard_map/ppermute | solution.py:40
  109.9 15.0 %collective-permute-start.13 = (f32[4,128,256]{2,1,0:T(8,128)S(1)}, f32[4,128,256]{2,1,0:T(8,128)S(1)}, u32[]{:S(2)}, u32[]{:S(2)}) collective-permute-start(f32[4,128,256]{2,1,0:T(8,128)S(1)} %pad_maximum_fusion.1.be0), channel_id=1, source_target_pairs={{0,1},{1,0},{2,3},{3,2},{4,5},{5,4},{6,7},{7,6},{8,9},{9,8},{10,11... | collective-permute-start | bytes 1572872 | tf_op jit(solution)/shard_map/ppermute | solution.py:40
  112.4 26.4 %collective-permute-start.9 = (f32[4,128,256]{2,1,0:T(8,128)S(1)}, f32[4,128,256]{2,1,0:T(8,128)S(1)}, u32[]{:S(2)}, u32[]{:S(2)}) collective-permute-start(f32[4,128,256]{2,1,0:T(8,128)S(1)} %pad_maximum_fusion.al0), channel_id=1, source_target_pairs={{0,12},{1,13},{2,14},{3,15},{4,8},{5,9},{6,10},{7,11},{8,4},{9,5},... | collective-permute-start | bytes 1572872 | tf_op jit(solution)/shard_map/ppermute | solution.py:40
  113.9 24.9 %collective-permute-start.8 = (f32[4,128,256]{2,1,0:T(8,128)S(1)}, f32[4,128,256]{2,1,0:T(8,128)S(1)}, u32[]{:S(2)}, u32[]{:S(2)}) collective-permute-start(f32[4,128,256]{2,1,0:T(8,128)S(1)} %pad_maximum_fusion.al0), channel_id=1, source_target_pairs={{0,8},{1,9},{2,10},{3,11},{4,12},{5,13},{6,14},{7,15},{8,0},{9,1},... | collective-permute-start | bytes 1572872 | tf_op jit(solution)/shard_map/ppermute | solution.py:40
  116.6 22.9 %collective-permute-start.7 = (f32[4,128,256]{2,1,0:T(8,128)S(1)}, f32[4,128,256]{2,1,0:T(8,128)S(1)}, u32[]{:S(2)}, u32[]{:S(2)}) collective-permute-start(f32[4,128,256]{2,1,0:T(8,128)S(1)} %pad_maximum_fusion.al0), channel_id=1, source_target_pairs={{0,4},{1,5},{2,6},{3,7},{4,0},{5,1},{6,2},{7,3},{8,12},{9,13},{10,... | collective-permute-start | bytes 1572872 | tf_op jit(solution)/shard_map/ppermute | solution.py:40
  (1 other events, 22.9 us)
